TPU v7x, 1024 devices: a whole 4x8x16 slice. The times are simulated.
1024 devices in a mesh: plate: 32 (over y_hi, z), tower: 8 (over y_lo, core), gz: 4 (over x).
Axes of the slice: x: 4, y: 8 (y_hi: 2, y_lo: 4; y = y_hi * 4 + y_lo), z: 16, core: 2. Of those that a mesh axis runs over, the one named last changes fastest.
Arguments:
- positions: float32 [32, 8, 4, 3, 128], P('plate', 'tower', 'gz'), may hold values from 0 to 1
- features: bfloat16 [32, 8, 4, 576, 128], P('plate', 'tower', 'gz'), may hold values from -6 to 6
- species: int32 [32, 8, 4, 128], P('plate', 'tower', 'gz'), may hold values from 0 to 5
- emb_table: bfloat16 [6, 64], replicated, may hold values from -4 to 4
- edges: int32 [32, 8, 4, 2, 512], P('plate', 'tower', 'gz'), may hold values from 0 to 1151, as said below
- edge_count: int32 [32, 8, 4], P('plate', 'tower', 'gz'), may hold values from 1 to 512, as said below
- w_first: bfloat16 [128, 328], replicated, may hold values from -0.3125 to 0.3125
- w_second: bfloat16 [64, 128], replicated, may hold values from -0.5 to 0.5
- w_out: bfloat16 [64], replicated, may hold values from -0.75 to 0.75
Outputs:
- forces: float32 [32, 8, 4, 3, 128], P('plate', 'tower', 'gz')
- edge_energy: float32 [32, 8, 4, 512], P('plate', 'tower', 'gz')
Inputs may be any that keep to these rules, and one draw needn't show every extreme that they name: `edges`: row 0 holds plate-set indices below 384; row 1 holds column-set indices below 1152. Slots at or beyond a box's edge_count are padding with arbitrary valid indices. `edge_count`: some box holds exactly 512 live edges in every draw.
All inputs are finite; a program needn't handle non-finite values.
Results may differ from a plain program's by a relative error of at most 0.011.
Values may be sent and summed in bfloat16 or wider, within the bound.
A program may use at most 32 MiB of HBM per device.

v0:
```python
import math

import jax
import jax.numpy as jnp
from jax import lax
from jax.sharding import PartitionSpec as P

RB = 8


RADIUS = 3.0
SOFTEN = 0.04


def with_halo(cells, sides, width):
    for axis, dim in sides:
        count = lax.axis_size(axis)
        head = lax.slice_in_dim(cells, 0, width, axis=dim)
        tail = lax.slice_in_dim(cells, cells.shape[dim] - width, cells.shape[dim], axis=dim)
        cells = jnp.concatenate(
            [
                lax.ppermute(tail, axis, [(i, (i + 1) % count) for i in range(count)]),
                cells,
                lax.ppermute(head, axis, [((i + 1) % count, i) for i in range(count)]),
            ],
            axis=dim,
        )
    return cells


def harmonics(unit_vec):
    cx, cy, cz = (unit_vec[0], unit_vec[1], unit_vec[2])
    root3 = math.sqrt(3.0)
    root15 = math.sqrt(15.0)
    root5 = math.sqrt(5.0)
    return jnp.stack(
        [
            jnp.ones_like(cx),
            root3 * cx,
            root3 * cy,
            root3 * cz,
            root15 * cx * cy,
            root15 * cy * cz,
            0.5 * root5 * (3.0 * cz * cz - 1.0),
            root15 * cx * cz,
            0.5 * root15 * (cx * cx - cy * cy),
        ]
    )


def pack_block(positions, features, species, emb_table):
    pos_hi = positions.astype(jnp.bfloat16)
    back = lax.optimization_barrier(pos_hi).astype(jnp.float32)
    pos_lo = (positions - back).astype(jnp.bfloat16)
    kinds = jnp.arange(emb_table.shape[0], dtype=jnp.int32)
    onehot = (species[..., None, :] == kinds[:, None]).astype(jnp.float32)
    emb = jnp.einsum("sc,...sa->...ca", emb_table.astype(jnp.float32), onehot).astype(jnp.bfloat16)
    return jnp.concatenate([features, emb, pos_hi, pos_lo], axis=-2)


def make_offsets(atoms):
    shifts = jnp.arange(3, dtype=jnp.float32) - 1.0
    plate_x = jnp.repeat(shifts, atoms)
    zeros_plate = jnp.zeros_like(plate_x)
    plate_off = jnp.stack([plate_x, zeros_plate, zeros_plate])
    column_y = jnp.repeat(jnp.repeat(shifts, 3), atoms)
    column_z = jnp.repeat(jnp.tile(shifts, 3), atoms)
    column_off = jnp.stack([jnp.zeros_like(column_y), column_y, column_z])
    return (plate_off, column_off)


def degree_sums(terms):
    return jnp.concatenate([terms[0], jnp.sum(terms[1:4], 0), jnp.sum(terms[4:9], 0)], 0)


def edge_model(coord_i, coord_j, feat_i, feat_j, emb_i, emb_j, w_first, w_second, w_out):
    width = emb_i.shape[0]
    delta = coord_j - coord_i
    dist2 = jnp.sum(delta * delta, 0) + SOFTEN
    dist = jnp.sqrt(dist2)
    harmonic = harmonics(delta / dist)
    orders = jnp.arange(1, RB + 1, dtype=jnp.float32)
    radial = jnp.sin(orders[:, None] * (math.pi / RADIUS) * dist[None, :]) / dist[None, :]
    envelope = jnp.square(jnp.maximum(1.0 - dist2 / (RADIUS * RADIUS), 0.0))
    proj_i = degree_sums(feat_i.astype(jnp.float32).reshape(9, width, -1) * harmonic[:, None, :])
    proj_j = degree_sums(feat_j.astype(jnp.float32).reshape(9, width, -1) * harmonic[:, None, :])
    inputs = jnp.concatenate(
        [radial, emb_i.astype(jnp.float32), emb_j.astype(jnp.float32), proj_i * proj_j], 0
    ).astype(jnp.bfloat16)
    hidden = jax.nn.silu(jnp.dot(w_first, inputs, preferred_element_type=jnp.float32)).astype(
        jnp.bfloat16
    )
    second_layer = jax.nn.silu(jnp.dot(w_second, hidden, preferred_element_type=jnp.float32))
    return envelope * jnp.sum(w_out.astype(jnp.float32)[:, None] * second_layer, 0)


def split_rows(picked, offsets, width):
    coord = (
        picked[10 * width : 10 * width + 3].astype(jnp.float32)
        + picked[10 * width + 3 : 10 * width + 6].astype(jnp.float32)
        + offsets
    )
    return (coord, picked[: 9 * width], picked[9 * width : 10 * width])


def device_pass(plate_rows, column_rows, edge_list, live_count, w_first, w_second, w_out):
    width = (plate_rows.shape[0] - 6) // 10
    atoms = plate_rows.shape[1] // 3
    plate_off, column_off = make_offsets(atoms)
    total = edge_list.shape[-1]
    block = min(1024, total)

    def step(index, carry):
        plate_part, column_part, energy = carry
        start = index * block
        left_index = edge_list[0]
        right_index = edge_list[1]
        slots = start + jnp.arange(block, dtype=jnp.int32)
        live_mask = (slots < live_count).astype(jnp.float32)
        coord_i, feat_i, emb_i = split_rows(
            jnp.take(plate_rows, left_index, axis=1), jnp.take(plate_off, left_index, axis=1), width
        )
        coord_j, feat_j, emb_j = split_rows(
            jnp.take(column_rows, right_index, axis=1),
            jnp.take(column_off, right_index, axis=1),
            width,
        )

        def energy_of(left_coord, right_coord):
            return live_mask * edge_model(
                left_coord, right_coord, feat_i, feat_j, emb_i, emb_j, w_first, w_second, w_out
            )

        values, pullback = jax.vjp(energy_of, coord_i, coord_j)
        grad_i, grad_j = pullback(jnp.ones_like(values))
        plate_part = plate_part.at[:, left_index].add(grad_i)
        column_part = column_part.at[:, right_index].add(grad_j)
        energy = values
        return (plate_part, column_part, energy)

    start_carry = (
        jnp.zeros((3, 3 * atoms), jnp.float32),
        jnp.zeros((3, 9 * atoms), jnp.float32),
        jnp.zeros((total,), jnp.float32),
    )
    upper = total // block
    return lax.fori_loop(0, upper, step, start_carry)


def shards(positions, features, species, emb_table, edges, edge_count, w_first, w_second, w_out):
    atoms = positions.shape[-1]
    packed = pack_block(positions, features, species, emb_table)
    rows_atom = packed.shape[3]
    plate_ext = with_halo(packed, (("plate", 0),), 1)
    plate_rows = jnp.transpose(plate_ext[:, 0, 0], (1, 0, 2)).reshape(rows_atom, 3 * atoms)
    column_ext = with_halo(packed, (("tower", 1), ("gz", 2)), 1)
    column_rows = jnp.transpose(column_ext[0].reshape(9, rows_atom, atoms), (1, 0, 2)).reshape(
        rows_atom, 9 * atoms
    )
    plate_part, column_part, energy = device_pass(
        plate_rows, column_rows, edges[0, 0, 0], edge_count[0, 0, 0], w_first, w_second, w_out
    )
    plate_slots = jnp.transpose(plate_part.reshape(3, 3, atoms), (1, 0, 2))
    column_slots = jnp.transpose(column_part.reshape(3, 3, 3, atoms), (1, 2, 0, 3))
    plate_back = with_halo(plate_slots, (("plate", 0),), 1)
    plate_mine = jnp.sum(plate_back[0::2], 0)
    column_back = with_halo(column_slots, (("tower", 0), ("gz", 1)), 1)
    column_mine = jnp.sum(column_back[0::2, 0::2], (0, 1))
    forces = -(plate_mine + column_mine)
    return (forces.reshape(1, 1, 1, 3, atoms), energy.reshape(1, 1, 1, -1))


def solution(mesh):
    placed = (
        P("plate", "tower", "gz", None, None),
        P("plate", "tower", "gz", None, None),
        P("plate", "tower", "gz", None),
        P(),
        P("plate", "tower", "gz", None, None),
        P("plate", "tower", "gz"),
        P(),
        P(),
        P(),
    )
    return jax.shard_map(
        shards,
        mesh=mesh,
        in_specs=placed,
        out_specs=(P("plate", "tower", "gz", None, None), P("plate", "tower", "gz", None)),
        check_vma=False,
    )
```

profile of v0, /device:TPU:6, one launch (start us, length us, event | category | flops | bytes accessed | tf_op | source)
XLA Modules:
  0.0 105.6 jit_solution(3610904727675471309)
XLA Ops:
  0.7 0.7 copy.56
  1.4 0.7 fusion.44
  2.1 0.9 fusion.6
  3.0 0.9 pad_maximum_fusion.4
  3.9 4.3 %collective-permute-start.4 = (bf16[1,1,1,646,128]{4,3,2,1,0:T(8,128)(2,1)S(1)}, bf16[1,1,1,646,128]{4,3,2,1,0:T(8,128)(2,1)S(1)}, u32[]{:S(2)}, u32[]{:S(2)}) collective-permute-start(bf16[1,1,1,646,128]{4,3,2,1,0:T(8,128)(2,1)S(1)} %pad_maximum_fusion.4), channel_id=1, source_target_pairs={{0,32},{32,64},{64,96},{96,128},{128,160},{160,192},{192,224},{224... | collective-permute-start | bytes 496136 | tf_op jit(solution)/shard_map/ppermute | solution.py:22
  8.2 21.1 %collective-permute-start.5 = (bf16[1,1,1,646,128]{4,3,2,1,0:T(8,128)(2,1)S(1)}, bf16[1,1,1,646,128]{4,3,2,1,0:T(8,128)(2,1)S(1)}, u32[]{:S(2)}, u32[]{:S(2)}) collective-permute-start(bf16[1,1,1,646,128]{4,3,2,1,0:T(8,128)(2,1)S(1)} %pad_maximum_fusion.4), channel_id=1, source_target_pairs={{32,0},{64,32},{96,64},{128,96},{160,128},{192,160},{224,192},{256... | collective-permute-start | bytes 496136 | tf_op jit(solution)/shard_map/ppermute | solution.py:24
  29.3 2.0 %collective-permute-start.1 = (bf16[1,1,1,646,128]{4,3,2,1,0:T(8,128)(2,1)S(1)}, bf16[1,1,1,646,128]{4,3,2,1,0:T(8,128)(2,1)S(1)}, u32[]{:S(2)}, u32[]{:S(2)}) collective-permute-start(bf16[1,1,1,646,128]{4,3,2,1,0:T(8,128)(2,1)S(1)} %pad_maximum_fusion.4), channel_id=1, source_target_pairs={{4,0},{8,4},{12,8},{16,12},{20,16},{24,20},{28,24},{0,28},{5,1},{9... | collective-permute-start | bytes 496136 | tf_op jit(solution)/shard_map/ppermute | solution.py:24
  31.3 2.4 %collective-permute-start = (bf16[1,1,1,646,128]{4,3,2,1,0:T(8,128)(2,1)S(1)}, bf16[1,1,1,646,128]{4,3,2,1,0:T(8,128)(2,1)S(1)}, u32[]{:S(2)}, u32[]{:S(2)}) collective-permute-start(bf16[1,1,1,646,128]{4,3,2,1,0:T(8,128)(2,1)S(1)} %pad_maximum_fusion.4), channel_id=1, source_target_pairs={{0,4},{4,8},{8,12},{12,16},{16,20},{20,24},{24,28},{28,0},{1,5},{5... | collective-permute-start | bytes 496136 | tf_op jit(solution)/shard_map/ppermute | solution.py:22
  33.7 0.8 fusion.70
  34.4 0.8 compare_select_fusion
  36.4 3.4 %collective-permute-done = bf16[1,1,1,646,128]{4,3,2,1,0:T(8,128)(2,1)S(1)} collective-permute-done((bf16[1,1,1,646,128]{4,3,2,1,0:T(8,128)(2,1)S(1)}, bf16[1,1,1,646,128]{4,3,2,1,0:T(8,128)(2,1)S(1)}, u32[]{:S(2)}, u32[]{:S(2)}) %collective-permute-start) | collective-permute-done | bytes 165408 | tf_op jit(solution)/shard_map/ppermute | solution.py:22
  39.7 1.0 pad_maximum_fusion.1
  40.7 2.7 %collective-permute-start.3 = (bf16[1,3,1,646,128]{4,3,2,1,0:T(8,128)(2,1)S(1)}, bf16[1,3,1,646,128]{4,3,2,1,0:T(8,128)(2,1)}, u32[]{:S(2)}, u32[]{:S(2)}) collective-permute-start(bf16[1,3,1,646,128]{4,3,2,1,0:T(8,128)(2,1)S(1)} %pad_maximum_fusion.1), channel_id=1, source_target_pairs={{1,0},{2,1},{3,2},{0,3},{5,4},{6,5},{7,6},{4,7},{9,8},{10,9},{11,1... | collective-permute-start | bytes 1488392 | tf_op jit(solution)/shard_map/ppermute | solution.py:24
  43.4 4.3 %collective-permute-start.2 = (bf16[1,3,1,646,128]{4,3,2,1,0:T(8,128)(2,1)S(1)}, bf16[1,3,1,646,128]{4,3,2,1,0:T(8,128)(2,1)}, u32[]{:S(2)}, u32[]{:S(2)}) collective-permute-start(bf16[1,3,1,646,128]{4,3,2,1,0:T(8,128)(2,1)S(1)} %pad_maximum_fusion.1), channel_id=1, source_target_pairs={{0,1},{1,2},{2,3},{3,0},{4,5},{5,6},{6,7},{7,4},{8,9},{9,10},{10,1... | collective-permute-start | bytes 1488392 | tf_op jit(solution)/shard_map/ppermute | solution.py:22
  49.7 1.0 gather_fusion.1
  50.9 4.6 %gather_fusion.3 = f32[512]{0:T(512)} fusion(f32[384]{0:T(512)S(1)} %broadcast_bitcast_fusion.2, s32[1024]{0:T(1024)S(1)} %pad_clamp_fusion), kind=kCustom, calls=%fused_computation.3 | custom fusion | bytes 6144 | tf_op jit(solution)/shard_map/while/body/eval_jaxpr/jit(_take)/gather | solution.py:121
  56.4 2.0 %gather_fusion.2 = bf16[512,646]{1,0:T(8,128)(2,1)S(1)} fusion(bf16[646,384]{0,1:T(8,128)(2,1)S(1)} %bitcast.88, s32[1024]{0:T(1024)S(1)} %pad_clamp_fusion), kind=kCustom, calls=%fused_computation.2 | custom fusion | bytes 1325056 | tf_op jit(solution)/shard_map/while/body/eval_jaxpr/jit(_take)/gather | solution.py:121
  58.4 1.1 %copy.38 = bf16[512,646]{0,1:T(8,128)(2,1)} copy(bf16[512,646]{1,0:T(8,128)(2,1)S(1)} %gather_fusion.2) | data formatting | bytes 1323008 | tf_op jit(solution)/shard_map/while/body/eval_jaxpr/jit(_take)/gather | solution.py:121
  59.5 1.8 %pad_maximum_fusion = bf16[1,3,3,646,128]{4,3,2,1,0:T(8,128)(2,1)S(1)} fusion(bf16[1,3,1,646,128]{4,3,2,1,0:T(8,128)(2,1)} %collective-permute-done.3, bf16[1,1,1,646,128]{4,3,2,1,0:T(8,128)(2,1)S(1)} %collective-permute-done.1, bf16[1,1,1,3,128]{4,3,2,1,0:T(4,128)(2,1)S(1)} %fusion.44, bf16[1,1,1,3,128]{4,3,2,1,0:T(4,128)(2,1)S(1)} %copy.56, ...), kind=kLoop, calls=%fused_computation.6 | loop fusion | flops 11907072 | bytes 2976768 | tf_op jit(solution)/shard_map/concatenate | solution.py:20
  61.3 0.9 copy.33
  62.2 2.0 %gather_fusion = bf16[512,646]{1,0:T(8,128)(2,1)S(1)} fusion(bf16[646,1152]{0,1:T(8,128)(2,1)S(1)} %bitcast.89, s32[1024]{0:T(1024)S(1)} %pad_clamp_fusion.1), kind=kCustom, calls=%fused_computation | custom fusion | bytes 1325056 | tf_op jit(solution)/shard_map/while/body/eval_jaxpr/jit(_take)/gather | solution.py:124
  64.5 0.8 copy-done.1
  70.2 2.4 %scatter_custom_fusion = f32[3,384]{0,1:T(8,128)S(1)} fusion(s32[512]{0:T(512)} %bitcast.106, f32[512,3]{1,0:T(8,128)S(1)} %copy.39, f32[]{:T(128)} %constant.110.clone.1), kind=kCustom, calls=%fused_computation.65 | custom fusion | flops 1536 | bytes 5120 | tf_op jit(solution)/shard_map/while/body/eval_jaxpr/scatter-add | solution.py:136
  72.7 1.9 %collective-permute-start.6 = (f32[1,3,128]{2,1,0:T(4,128)S(1)}, f32[1,3,128]{2,1,0:T(4,128)S(1)}, u32[]{:S(2)}, u32[]{:S(2)}) collective-permute-start(f32[1,3,128]{2,1,0:T(4,128)S(1)} %get-tuple-element.75), channel_id=1, source_target_pairs={{0,32},{32,64},{64,96},{96,128},{128,160},{160,192},{192,224},{224... | collective-permute-start | bytes 4616 | tf_op jit(solution)/shard_map/ppermute | solution.py:22
  74.6 9.9 %collective-permute-start.7 = (f32[1,3,128]{2,1,0:T(4,128)S(1)}, f32[1,3,128]{2,1,0:T(4,128)S(1)}, u32[]{:S(2)}, u32[]{:S(2)}) collective-permute-start(f32[1,3,128]{2,1,0:T(4,128)S(1)} %get-tuple-element.76), channel_id=1, source_target_pairs={{32,0},{64,32},{96,64},{128,96},{160,128},{192,160},{224,192},{256... | collective-permute-start | bytes 4616 | tf_op jit(solution)/shard_map/ppermute | solution.py:24
  84.6 2.5 %scatter_custom_fusion.1 = f32[3,1152]{0,1:T(8,128)S(1)} fusion(s32[512]{0:T(512)} %bitcast.104, f32[512,3]{1,0:T(8,128)S(1)} %copy.42, f32[]{:T(128)} %constant.110.clone.1), kind=kCustom, calls=%fused_computation.44 | custom fusion | flops 1536 | bytes 14336 | tf_op jit(solution)/shard_map/while/body/eval_jaxpr/scatter-add | solution.py:137
  87.3 1.9 %collective-permute-start.8 = (f32[1,3,3,128]{3,2,1,0:T(4,128)S(1)}, f32[1,3,3,128]{3,2,1,0:T(4,128)S(1)}, u32[]{:S(2)}, u32[]{:S(2)}) collective-permute-start(f32[1,3,3,128]{3,2,1,0:T(4,128)S(1)} %get-tuple-element.65), channel_id=1, source_target_pairs={{0,4},{4,8},{8,12},{12,16},{16,20},{20,24},{24,28},{28,0},{1,5},{5... | collective-permute-start | bytes 13832 | tf_op jit(solution)/shard_map/ppermute | solution.py:22
  89.3 5.4 %collective-permute-start.9 = (f32[1,3,3,128]{3,2,1,0:T(4,128)S(1)}, f32[1,3,3,128]{3,2,1,0:T(4,128)S(1)}, u32[]{:S(2)}, u32[]{:S(2)}) collective-permute-start(f32[1,3,3,128]{3,2,1,0:T(4,128)S(1)} %get-tuple-element.66), channel_id=1, source_target_pairs={{4,0},{8,4},{12,8},{16,12},{20,16},{24,20},{28,24},{0,28},{5,1},{9... | collective-permute-start | bytes 13832 | tf_op jit(solution)/shard_map/ppermute | solution.py:24
  95.3 0.7 collective-permute-done.9
  96.1 1.9 %collective-permute-start.10 = (f32[5,1,3,128]{3,2,1,0:T(4,128)S(1)}, f32[5,1,3,128]{3,2,1,0:T(4,128)S(1)}, u32[]{:S(2)}, u32[]{:S(2)}) collective-permute-start(f32[5,1,3,128]{3,2,1,0:T(4,128)S(1)} %get-tuple-element.63), channel_id=1, source_target_pairs={{0,1},{1,2},{2,3},{3,0},{4,5},{5,6},{6,7},{7,4},{8,9},{9,10},{10,1... | collective-permute-start | bytes 23048 | tf_op jit(solution)/shard_map/ppermute | solution.py:22
  98.0 3.9 %collective-permute-start.11 = (f32[5,1,3,128]{3,2,1,0:T(4,128)S(1)}, f32[5,1,3,128]{3,2,1,0:T(4,128)S(1)}, u32[]{:S(2)}, u32[]{:S(2)}) collective-permute-start(f32[5,1,3,128]{3,2,1,0:T(4,128)S(1)} %get-tuple-element.64), channel_id=1, source_target_pairs={{1,0},{2,1},{3,2},{0,3},{5,4},{6,5},{7,6},{4,7},{9,8},{10,9},{11,1... | collective-permute-start | bytes 23048 | tf_op jit(solution)/shard_map/ppermute | solution.py:24
  102.0 2.7 %collective-permute-done.11 = f32[5,1,3,128]{3,2,1,0:T(4,128)S(1)} collective-permute-done((f32[5,1,3,128]{3,2,1,0:T(4,128)S(1)}, f32[5,1,3,128]{3,2,1,0:T(4,128)S(1)}, u32[]{:S(2)}, u32[]{:S(2)}) %collective-permute-start.11) | collective-permute-done | bytes 7712 | tf_op jit(solution)/shard_map/ppermute | solution.py:24
  (109 shorter events, 10.0 us)
Async XLA Ops:
  0.6 66.8 %copy-start = (bf16[128,328]{0,1:T(8,128)(2,1)S(1)}, bf16[128,328]{0,1:T(8,128)(2,1)}, u32[]{:S(2)}) copy-start(bf16[128,328]{0,1:T(8,128)(2,1)} %param.15) | copy-start | bytes 251908
  0.6 48.3 %copy-start.10 = (bf16[64]{0:T(256)(128)(2,1)S(1)}, bf16[64]{0:T(256)(128)(2,1)}, u32[]{:S(2)}) copy-start(bf16[64]{0:T(256)(128)(2,1)} %param.17) | copy-start | bytes 388
  3.9 52.2 %collective-permute-start.4 = (bf16[1,1,1,646,128]{4,3,2,1,0:T(8,128)(2,1)S(1)}, bf16[1,1,1,646,128]{4,3,2,1,0:T(8,128)(2,1)S(1)}, u32[]{:S(2)}, u32[]{:S(2)}) collective-permute-start(bf16[1,1,1,646,128]{4,3,2,1,0:T(8,128)(2,1)S(1)} %pad_maximum_fusion.4), channel_id=1, source_target_pairs={{0,32},{32,64},{64,96},{96,128},{128,160},{160,192},{192,224},{224... | collective-permute-start | bytes 496136 | tf_op jit(solution)/shard_map/ppermute | solution.py:22
  8.2 47.9 %collective-permute-start.5 = (bf16[1,1,1,646,128]{4,3,2,1,0:T(8,128)(2,1)S(1)}, bf16[1,1,1,646,128]{4,3,2,1,0:T(8,128)(2,1)S(1)}, u32[]{:S(2)}, u32[]{:S(2)}) collective-permute-start(bf16[1,1,1,646,128]{4,3,2,1,0:T(8,128)(2,1)S(1)} %pad_maximum_fusion.4), channel_id=1, source_target_pairs={{32,0},{64,32},{96,64},{128,96},{160,128},{192,160},{224,192},{256... | collective-permute-start | bytes 496136 | tf_op jit(solution)/shard_map/ppermute | solution.py:24
  29.3 7.1 %collective-permute-start.1 = (bf16[1,1,1,646,128]{4,3,2,1,0:T(8,128)(2,1)S(1)}, bf16[1,1,1,646,128]{4,3,2,1,0:T(8,128)(2,1)S(1)}, u32[]{:S(2)}, u32[]{:S(2)}) collective-permute-start(bf16[1,1,1,646,128]{4,3,2,1,0:T(8,128)(2,1)S(1)} %pad_maximum_fusion.4), channel_id=1, source_target_pairs={{4,0},{8,4},{12,8},{16,12},{20,16},{24,20},{28,24},{0,28},{5,1},{9... | collective-permute-start | bytes 496136 | tf_op jit(solution)/shard_map/ppermute | solution.py:24
  31.3 8.5 %collective-permute-start = (bf16[1,1,1,646,128]{4,3,2,1,0:T(8,128)(2,1)S(1)}, bf16[1,1,1,646,128]{4,3,2,1,0:T(8,128)(2,1)S(1)}, u32[]{:S(2)}, u32[]{:S(2)}) collective-permute-start(bf16[1,1,1,646,128]{4,3,2,1,0:T(8,128)(2,1)S(1)} %pad_maximum_fusion.4), channel_id=1, source_target_pairs={{0,4},{4,8},{8,12},{12,16},{16,20},{20,24},{24,28},{28,0},{1,5},{5... | collective-permute-start | bytes 496136 | tf_op jit(solution)/shard_map/ppermute | solution.py:22
  35.2 20.3 %copy-start.3 = (s32[512,1]{0,1:T(1,128)}, s32[512,1]{0,1:T(1,128)S(1)}, u32[]{:S(2)}) copy-start(s32[512,1]{0,1:T(1,128)S(1)} %get-tuple-element.81) | copy-start | bytes 6148
  35.2 20.3 %copy-start.4 = (s32[512,1]{0,1:T(1,128)}, s32[512,1]{0,1:T(1,128)S(1)}, u32[]{:S(2)}) copy-start(s32[512,1]{0,1:T(1,128)S(1)} %get-tuple-element.82) | copy-start | bytes 6148
  40.7 18.8 %collective-permute-start.3 = (bf16[1,3,1,646,128]{4,3,2,1,0:T(8,128)(2,1)S(1)}, bf16[1,3,1,646,128]{4,3,2,1,0:T(8,128)(2,1)}, u32[]{:S(2)}, u32[]{:S(2)}) collective-permute-start(bf16[1,3,1,646,128]{4,3,2,1,0:T(8,128)(2,1)S(1)} %pad_maximum_fusion.1), channel_id=1, source_target_pairs={{1,0},{2,1},{3,2},{0,3},{5,4},{6,5},{7,6},{4,7},{9,8},{10,9},{11,1... | collective-permute-start | bytes 1488392 | tf_op jit(solution)/shard_map/ppermute | solution.py:24
  43.4 16.1 %collective-permute-start.2 = (bf16[1,3,1,646,128]{4,3,2,1,0:T(8,128)(2,1)S(1)}, bf16[1,3,1,646,128]{4,3,2,1,0:T(8,128)(2,1)}, u32[]{:S(2)}, u32[]{:S(2)}) collective-permute-start(bf16[1,3,1,646,128]{4,3,2,1,0:T(8,128)(2,1)S(1)} %pad_maximum_fusion.1), channel_id=1, source_target_pairs={{0,1},{1,2},{2,3},{3,0},{4,5},{5,6},{6,7},{7,4},{8,9},{9,10},{10,1... | collective-permute-start | bytes 1488392 | tf_op jit(solution)/shard_map/ppermute | solution.py:22
  49.5 6.6 %copy-start.2 = (bf16[1,1,1,576,128]{4,3,2,1,0:T(8,128)(2,1)S(1)}, bf16[1,1,1,576,128]{4,3,2,1,0:T(8,128)(2,1)}, u32[]{:S(2)}) copy-start(bf16[1,1,1,576,128]{4,3,2,1,0:T(8,128)(2,1)} %param.10) | copy-start | bytes 442372
  62.2 2.3 %copy-start.6 = (pred[512]{0:T(512)(128)(4,1)S(1)}, pred[512]{0:T(512)(128)(4,1)}, u32[]{:S(2)}) copy-start(pred[512]{0:T(512)(128)(4,1)} %compare_and_fusion.1) | copy-start | bytes 1540
  62.2 2.3 %copy-start.7 = (pred[512]{0:T(512)(128)(4,1)S(1)}, pred[512]{0:T(512)(128)(4,1)}, u32[]{:S(2)}) copy-start(pred[512]{0:T(512)(128)(4,1)} %compare_and_fusion) | copy-start | bytes 1540
  64.2 1.1 %copy-start.1 = (bf16[512,646]{0,1:T(8,128)(2,1)S(1)}, bf16[512,646]{0,1:T(8,128)(2,1)}, u32[]{:S(2)}) copy-start(bf16[512,646]{0,1:T(8,128)(2,1)} %copy.38) | copy-start | bytes 1984516
  65.5 0.7 copy-start.5
  66.6 0.6 copy-start.8
  66.8 1.0 copy-start.9
  66.8 1.0 copy-start.11
  72.7 22.6 %collective-permute-start.6 = (f32[1,3,128]{2,1,0:T(4,128)S(1)}, f32[1,3,128]{2,1,0:T(4,128)S(1)}, u32[]{:S(2)}, u32[]{:S(2)}) collective-permute-start(f32[1,3,128]{2,1,0:T(4,128)S(1)} %get-tuple-element.75), channel_id=1, source_target_pairs={{0,32},{32,64},{64,96},{96,128},{128,160},{160,192},{192,224},{224... | collective-permute-start | bytes 4616 | tf_op jit(solution)/shard_map/ppermute | solution.py:22
  74.6 20.7 %collective-permute-start.7 = (f32[1,3,128]{2,1,0:T(4,128)S(1)}, f32[1,3,128]{2,1,0:T(4,128)S(1)}, u32[]{:S(2)}, u32[]{:S(2)}) collective-permute-start(f32[1,3,128]{2,1,0:T(4,128)S(1)} %get-tuple-element.76), channel_id=1, source_target_pairs={{32,0},{64,32},{96,64},{128,96},{160,128},{192,160},{224,192},{256... | collective-permute-start | bytes 4616 | tf_op jit(solution)/shard_map/ppermute | solution.py:24
  87.3 8.0 %collective-permute-start.8 = (f32[1,3,3,128]{3,2,1,0:T(4,128)S(1)}, f32[1,3,3,128]{3,2,1,0:T(4,128)S(1)}, u32[]{:S(2)}, u32[]{:S(2)}) collective-permute-start(f32[1,3,3,128]{3,2,1,0:T(4,128)S(1)} %get-tuple-element.65), channel_id=1, source_target_pairs={{0,4},{4,8},{8,12},{12,16},{16,20},{20,24},{24,28},{28,0},{1,5},{5... | collective-permute-start | bytes 13832 | tf_op jit(solution)/shard_map/ppermute | solution.py:22
  89.3 6.8 %collective-permute-start.9 = (f32[1,3,3,128]{3,2,1,0:T(4,128)S(1)}, f32[1,3,3,128]{3,2,1,0:T(4,128)S(1)}, u32[]{:S(2)}, u32[]{:S(2)}) collective-permute-start(f32[1,3,3,128]{3,2,1,0:T(4,128)S(1)} %get-tuple-element.66), channel_id=1, source_target_pairs={{4,0},{8,4},{12,8},{16,12},{20,16},{24,20},{28,24},{0,28},{5,1},{9... | collective-permute-start | bytes 13832 | tf_op jit(solution)/shard_map/ppermute | solution.py:24
  96.1 6.0 %collective-permute-start.10 = (f32[5,1,3,128]{3,2,1,0:T(4,128)S(1)}, f32[5,1,3,128]{3,2,1,0:T(4,128)S(1)}, u32[]{:S(2)}, u32[]{:S(2)}) collective-permute-start(f32[5,1,3,128]{3,2,1,0:T(4,128)S(1)} %get-tuple-element.63), channel_id=1, source_target_pairs={{0,1},{1,2},{2,3},{3,0},{4,5},{5,6},{6,7},{7,4},{8,9},{9,10},{10,1... | collective-permute-start | bytes 23048 | tf_op jit(solution)/shard_map/ppermute | solution.py:22
  98.0 6.8 %collective-permute-start.11 = (f32[5,1,3,128]{3,2,1,0:T(4,128)S(1)}, f32[5,1,3,128]{3,2,1,0:T(4,128)S(1)}, u32[]{:S(2)}, u32[]{:S(2)}) collective-permute-start(f32[5,1,3,128]{3,2,1,0:T(4,128)S(1)} %get-tuple-element.64), channel_id=1, source_target_pairs={{1,0},{2,1},{3,2},{0,3},{5,4},{6,5},{7,6},{4,7},{9,8},{10,9},{11,1... | collective-permute-start | bytes 23048 | tf_op jit(solution)/shard_map/ppermute | solution.py:24
where the time goes:
time: 106 us
  starting transfers between devices  61.9 us (58%)
  local copies, waits for them, and re-layouts  18.2 us (17%)
  other arithmetic  14.7 us (14%)
  waiting for transfers between devices  6.84 us (6%)
  matrix products  2.02 us (2%)
  between operations  1.9 us (2%)
    ppermute x6, starting transfers between devices, with_halo(): lax.ppermute(head, axis, [((i + 1) % count, i) for i in range(count)])  45.1 us
    ppermute x6, starting transfers between devices, with_halo(): lax.ppermute(tail, axis, [(i, (i + 1) % count) for i in range(count)])  16.7 us
    gather x1, local copies, waits for them, and re-layouts, step(): jnp.take(plate_off, left_index, axis=1)  4.65 us
    unnamed x30, local copies, waits for them, and re-layouts  3.51 us
    ppermute x6, waiting for transfers between devices, with_halo(): lax.ppermute(head, axis, [((i + 1) % count, i) for i in range(count)])  3.44 us
    ppermute x6, waiting for transfers between devices, with_halo(): lax.ppermute(tail, axis, [(i, (i + 1) % count) for i in range(count)])  3.4 us
    gather x2, local copies, waits for them, and re-layouts, step(): jnp.take(plate_rows, left_index, axis=1)  3.11 us
    concatenate x4, other arithmetic, with_halo(): jnp.concatenate([lax.ppermute(tail, axis, [(i, (i + 1) % count) for i in...  2.75 us
  transfers between devices with their start and end apart: 12, of which 3 were waited for; matrix products, arithmetic and copies ran while one was open for 17% of the time, Pallas kernels for 0%

commit v1 on v0

v1 whole, which is shorter than its diff:
```python
import math

import jax
import jax.numpy as jnp
from jax import lax
from jax.experimental import pallas as pl
from jax.experimental.pallas import tpu as pltpu
from jax.sharding import PartitionSpec as P

ATOMS = 128
EDGES = 512
CH = 64
LAT = 128
RB = 8
ROWS = 9 * CH
HALF = ROWS // 2
RADIUS = 3.0
SOFTEN = 0.04
F32 = jnp.float32
BF16 = jnp.bfloat16

NSLOT = 10


def dot(a, b):
    return lax.dot_general(a, b, (((1,), (0,)), ((), ())), preferred_element_type=F32)


def dot_nt(a, b):
    return lax.dot_general(a, b, (((1,), (1,)), ((), ())), preferred_element_type=F32)


def sin_cos_pi(t):
    turns = jnp.floor(t + 0.5)
    x = (t - turns) * math.pi
    parity = turns - 2.0 * jnp.floor(turns * 0.5)
    sign = 1.0 - 2.0 * parity
    y = x * x
    s = -1.0 / 39916800.0
    for c in (1.0 / 362880.0, -1.0 / 5040.0, 1.0 / 120.0, -1.0 / 6.0, 1.0):
        s = s * y + c
    c_ = 1.0 / 479001600.0
    for c in (-1.0 / 3628800.0, 1.0 / 40320.0, -1.0 / 720.0, 1.0 / 24.0, -0.5, 1.0):
        c_ = c_ * y + c
    return sign * s * x, sign * c_


def kernel(
    pos_ref,
    feat_ref,
    spec_ref,
    edges_ref,
    count_ref,
    table_ref,
    w1_ref,
    w2_ref,
    wout_ref,
    force_ref,
    energy_ref,
    fslot,
    mown,
    mslot,
    ohp,
    ohc,
    gi,
    gj,
    si,
    sj,
    yb,
    xbuf,
    wtmp,
    wp,
    wpt,
    w2t,
    tmat,
    gbuf,
    rad,
    pout,
    pslot,
    msend,
    mrecv,
    fsend,
    frecv,
    psend,
    precv,
):
    n_plate, n_tower, n_gz = (lax.axis_size(a) for a in ("plate", "tower", "gz"))
    p, t, g = (lax.axis_index(a) for a in ("plate", "tower", "gz"))
    odd = lax.rem(t, 2)
    partner = t + 1 - 2 * odd
    outward = lax.rem(t + 2 * odd - 1 + n_tower, n_tower)
    g_up, g_dn = lax.rem(g + 1, n_gz), lax.rem(g + n_gz - 1, n_gz)
    p_up, p_dn = lax.rem(p + 1, n_plate), lax.rem(p + n_plate - 1, n_plate)

    def dev(pp, tt, gg):
        return {"plate": pp, "tower": tt, "gz": gg}

    dest = [
        dev(p, t, g_up), dev(p, t, g_dn), dev(p, partner, g), dev(p, outward, g),
        dev(p, partner, g_up), dev(p, partner, g_dn), dev(p, outward, g_up), dev(p, outward, g_dn),
        dev(p_up, t, g), dev(p_dn, t, g),
    ]
    home = [dest[k] for k in (1, 0, 2, 3, 5, 4, 7, 6, 9, 8)]

    barrier = pltpu.get_barrier_semaphore()
    for d in dest:
        pl.semaphore_signal(barrier, inc=1, device_id=d, device_id_type=pl.DeviceIdType.MESH)

    pos = pos_ref[...]
    hi = pos.astype(BF16).astype(F32)
    lo = (pos - hi).astype(BF16).astype(F32)
    rad[...] = jnp.zeros_like(rad)
    rad[0:3, 0:ATOMS] = hi
    rad[3:6, 0:ATOMS] = lo
    rad[6:7, 0:ATOMS] = spec_ref[...].astype(F32)
    mown[...] = rad[:, 0:ATOMS].astype(BF16)

    def remote(src, dst, ssem, rsem, to):
        return pltpu.make_async_remote_copy(
            src_ref=src,
            dst_ref=dst,
            send_sem=ssem,
            recv_sem=rsem,
            device_id=to,
            device_id_type=pl.DeviceIdType.MESH,
        )

    meta = [remote(mown, mslot.at[k], msend.at[k], mrecv.at[k], dest[k]) for k in range(NSLOT)]
    top, low = pl.ds(0, HALF), pl.ds(HALF, HALF)

    def feature(n, src, slot, to, part=None):
        dst = fslot.at[slot]
        if part is not None:
            src, dst = src.at[part], dst.at[part]
        return remote(src, dst, fsend.at[n], frecv.at[n], to)

    f_g_up = feature(0, feat_ref, 0, dest[0])
    f_g_dn = feature(1, feat_ref, 1, dest[1])
    f_part = feature(2, feat_ref, 2, dest[2])
    f_out = [feature(3, feat_ref, 3, dest[3], top), feature(4, feat_ref, 3, dest[3], low)]
    f_p_up = feature(5, feat_ref, 8, dest[8])
    f_p_dn = feature(6, feat_ref, 9, dest[9])
    r_part = [feature(7, fslot.at[0], 4, dest[2]), feature(8, fslot.at[1], 5, dest[2])]
    r_up = [feature(9, fslot.at[3], 6, dest[0], top), feature(10, fslot.at[3], 6, dest[0], low)]
    r_dn = [feature(11, fslot.at[3], 7, dest[1], top), feature(12, fslot.at[3], 7, dest[1], low)]

    pl.semaphore_wait(barrier, NSLOT)
    for c in meta:
        c.start()
    for c in (f_out[0], f_out[1], f_g_up, f_g_dn, f_p_up, f_p_dn, f_part):
        c.start()

    left, right = edges_ref[0:1, :], edges_ref[1:2, :]
    row = lax.broadcasted_iota(jnp.int32, (3 * ATOMS, EDGES), 0)
    ohp[...] = jnp.where(row == left, 1.0, 0.0).astype(BF16)
    for k, u in enumerate((1, 2 - 2 * odd, 2 * odd)):
        shifted = right - 3 * ATOMS * u
        ohc[3 * ATOMS * k : 3 * ATOMS * (k + 1), :] = jnp.where(row == shifted, 1.0, 0.0).astype(BF16)

    tmat[...] = jnp.zeros_like(tmat)
    tmat[0:6, 0:CH] = table_ref[...].astype(F32)
    tmat[6:7, 0:CH] = wout_ref[...].astype(F32)
    turned = jnp.transpose(tmat[...])
    embt = turned[0:CH, :].astype(BF16)
    wout = turned[0:CH, 6:7]
    wtmp[...] = jnp.zeros_like(wtmp)
    wtmp[:, 0 : RB + 5 * CH] = w1_ref[...].astype(F32)
    wfull = pltpu.roll(wtmp[...], 6 * CH - RB, 1)
    wp[...] = wfull.astype(BF16)
    wpt[...] = jnp.transpose(wfull).astype(BF16)
    w2t[...] = jnp.transpose(w2_ref[...].astype(F32)).astype(BF16)

    f_out[0].wait_recv()
    r_up[0].start()
    r_dn[0].start()
    f_out[1].wait_recv()
    r_up[1].start()
    r_dn[1].start()
    f_g_up.wait_recv()
    r_part[0].start()
    f_g_dn.wait_recv()
    r_part[1].start()

    for c in meta:
        c.wait_recv()
    mi = dot(jnp.concatenate([mslot[8], mown[...], mslot[9]], 1), ohp[...])
    order = [mslot[0], mown[...], mslot[1], mslot[4], mslot[2], mslot[5], mslot[6], mslot[3], mslot[7]]
    mj = dot(jnp.concatenate(order, 1), ohc[...])
    off_i = jnp.where(left < ATOMS, -1.0, jnp.where(left < 2 * ATOMS, 0.0, 1.0))
    off_u = jnp.where(right < 3 * ATOMS, 0, jnp.where(right < 6 * ATOMS, 1, 2))
    rest = right - 3 * ATOMS * off_u
    off_v = jnp.where(rest < ATOMS, -1.0, jnp.where(rest < 2 * ATOMS, 0.0, 1.0))
    dx = (mj[0:1] + mj[3:4]) - (mi[0:1] + mi[3:4] + off_i)
    dy = (mj[1:2] + mj[4:5] + (off_u.astype(F32) - 1.0)) - (mi[1:2] + mi[4:5])
    dz = (mj[2:3] + mj[5:6] + off_v) - (mi[2:3] + mi[5:6])
    r2 = dx * dx + dy * dy + dz * dz + SOFTEN
    r = jnp.sqrt(r2)
    inv = 1.0 / r
    nx, ny, nz = dx * inv, dy * inv, dz * inv
    root3, root5, root15 = math.sqrt(3.0), math.sqrt(5.0), math.sqrt(15.0)
    harm = (
        root3 * nx, root3 * ny, root3 * nz, root15 * nx * ny, root15 * ny * nz,
        0.5 * root5 * (3.0 * nz * nz - 1.0), root15 * nx * nz, 0.5 * root15 * (nx * nx - ny * ny),
    )
    for m in range(8):
        yb[m] = jnp.broadcast_to(harm[m], (8, EDGES))
    orders = (lax.broadcasted_iota(jnp.int32, (RB, EDGES), 0) + 1).astype(F32)
    sin_b, cos_b = sin_cos_pi(orders * (1.0 / RADIUS) * r)
    radial = sin_b * inv
    slope = (orders * (math.pi / RADIUS) * cos_b - radial) * inv
    live = jnp.where(lax.broadcasted_iota(jnp.int32, (1, EDGES), 1) < count_ref[0, 0], 1.0, 0.0)
    gap = jnp.maximum(1.0 - r2 * (1.0 / (RADIUS * RADIUS)), 0.0)
    env = live * gap * gap
    kinds = lax.broadcasted_iota(jnp.int32, (LAT, EDGES), 0)
    for k, m in enumerate((mi, mj)):
        pick = jnp.where(kinds == m[6:7].astype(jnp.int32), 1.0, 0.0).astype(BF16)
        xbuf[CH * k : CH * (k + 1), :] = dot(embt, pick).astype(BF16)
    xbuf[5 * CH : 6 * CH - 16, :] = jnp.zeros((CH - 16, EDGES), BF16)
    xbuf[6 * CH - 16 : 6 * CH, :] = jnp.concatenate([jnp.zeros_like(radial), radial], 0).astype(BF16)

    f_part.wait_recv()
    for c in (*r_part, *r_up, *r_dn):
        c.wait_recv()
    order = [fslot[0], feat_ref[...], fslot[1], fslot[4], fslot[2], fslot[5], fslot[6], fslot[3], fslot[7]]
    gj[...] = dot(jnp.concatenate(order, 1), ohc[...])
    f_p_up.wait_recv()
    f_p_dn.wait_recv()
    gi[...] = dot(jnp.concatenate([fslot[8], feat_ref[...], fslot[9]], 1), ohp[...])

    def rows_of(ref, m, k):
        return ref[m * CH + 8 * k : m * CH + 8 * k + 8, :]

    for k2 in range(CH // 16):
        prods = [[], [], []]
        for k in (2 * k2, 2 * k2 + 1):
            sums = []
            for ref in (gi, gj):
                one = [rows_of(ref, m, k) * yb[m - 1] for m in range(1, 9)]
                sums.append((
                    rows_of(ref, 0, k),
                    one[0] + one[1] + one[2],
                    one[3] + one[4] + one[5] + one[6] + one[7],
                ))
            for l in range(3):
                si[l * CH + 8 * k : l * CH + 8 * k + 8, :] = sums[0][l]
                sj[l * CH + 8 * k : l * CH + 8 * k + 8, :] = sums[1][l]
                prods[l].append(sums[0][l] * sums[1][l])
        for l in range(3):
            start = (2 + l) * CH + 16 * k2
            xbuf[start : start + 16, :] = jnp.concatenate(prods[l], 0).astype(BF16)
    z1 = dot(wp[...], xbuf[...])
    sig1 = 1.0 / (1.0 + jnp.exp(-z1))
    z2 = dot(w2_ref[...], (z1 * sig1).astype(BF16))
    sig2 = 1.0 / (1.0 + jnp.exp(-z2))
    u = jnp.sum(wout * (z2 * sig2), 0, keepdims=True)
    energy_ref[...] = env * u

    dz2 = (wout * env) * (sig2 * (1.0 + z2 * (1.0 - sig2)))
    dh = dot(w2t[...], dz2.astype(BF16)).astype(BF16).astype(F32)
    dz1 = dh * (sig1 * (1.0 + z1 * (1.0 - sig1)))
    dxv = dot(wpt[...], dz1.astype(BF16)).astype(BF16).astype(F32)
    acc = [jnp.zeros((8, EDGES), F32) for _ in range(8)]
    for k in range(CH // 8):
        for l, ms in ((1, (1, 2, 3)), (2, (4, 5, 6, 7, 8))):
            at = slice(l * CH + 8 * k, l * CH + 8 * k + 8)
            dq = dxv[2 * CH + at.start : 2 * CH + at.stop, :]
            di, dj = dq * sj[at, :], dq * si[at, :]
            for m in ms:
                acc[m - 1] = acc[m - 1] + di * rows_of(gi, m, k) + dj * rows_of(gj, m, k)
    h1, h2, h3, h4, h5, h6, h7, h8 = (jnp.sum(a, 0, keepdims=True) for a in acc)
    ax = root3 * h1 + root15 * (ny * h4 + nz * h7 + nx * h8)
    ay = root3 * h2 + root15 * (nx * h4 + nz * h5 - ny * h8)
    az = root3 * h3 + root15 * (ny * h5 + nx * h7) + (3.0 * root5) * nz * h6
    dr = jnp.sum(dxv[6 * CH - RB : 6 * CH, :] * slope, 0, keepdims=True)
    dr = dr - (ax * nx + ay * ny + az * nz) * inv
    denv = live * u * (2.0 * gap) * (-1.0 / (RADIUS * RADIUS))
    scale = dr * inv + 2.0 * denv
    gbuf[...] = jnp.zeros_like(gbuf)
    gbuf[0:1, :] = ax * inv + dx * scale
    gbuf[1:2, :] = ay * inv + dy * scale
    gbuf[2:3, :] = az * inv + dz * scale

    grad = gbuf[...]
    g_hi = grad.astype(BF16).astype(F32)
    both = jnp.concatenate([g_hi, grad - g_hi], 0).astype(BF16)
    part_p = dot_nt(both, ohp[...])
    part_p = part_p[0:8] + part_p[8:16]
    part_c = dot_nt(both, ohc[...])
    part_c = -(part_c[0:8] + part_c[8:16])

    def lanes(a, k):
        return a[:, k * ATOMS : (k + 1) * ATOMS]

    for slot, k in enumerate((0, 2, 4, 7, 3, 5, 6, 8)):
        pout[slot] = lanes(part_c, k)
    pout[8] = lanes(part_p, 0)
    pout[9] = lanes(part_p, 2)
    back = [remote(pout.at[k], pslot.at[k], psend.at[k], precv.at[k], home[k]) for k in range(NSLOT)]
    for c in back:
        c.start()
    total = lanes(part_p, 1) + lanes(part_c, 1)
    for c in (*meta, f_g_up, f_g_dn, f_part, *f_out, f_p_up, f_p_dn, *r_part, *r_up, *r_dn):
        c.wait_send()
    for k, c in enumerate(back):
        c.wait_recv()
        total = total + pslot[k]
    force_ref[...] = total[0:3, :]
    for c in back:
        c.wait_send()


def shards(positions, features, species, emb_table, edges, edge_count, w_first, w_second, w_out):
    vmem = pl.BlockSpec(memory_space=pltpu.VMEM)
    dma = pltpu.SemaphoreType.DMA
    forces, energy = pl.pallas_call(
        kernel,
        name="edge_forces",
        out_shape=(jax.ShapeDtypeStruct((3, ATOMS), F32), jax.ShapeDtypeStruct((1, EDGES), F32)),
        in_specs=[vmem, vmem, vmem, vmem, pl.BlockSpec(memory_space=pltpu.SMEM), vmem, vmem, vmem, vmem],
        out_specs=(vmem, vmem),
        scratch_shapes=[
            pltpu.VMEM((NSLOT, ROWS, ATOMS), BF16),
            pltpu.VMEM((16, ATOMS), BF16),
            pltpu.VMEM((NSLOT, 16, ATOMS), BF16),
            pltpu.VMEM((3 * ATOMS, EDGES), BF16),
            pltpu.VMEM((9 * ATOMS, EDGES), BF16),
            pltpu.VMEM((ROWS, EDGES), F32),
            pltpu.VMEM((ROWS, EDGES), F32),
            pltpu.VMEM((3 * CH, EDGES), F32),
            pltpu.VMEM((3 * CH, EDGES), F32),
            pltpu.VMEM((8, 8, EDGES), F32),
            pltpu.VMEM((6 * CH, EDGES), BF16),
            pltpu.VMEM((LAT, 6 * CH), F32),
            pltpu.VMEM((LAT, 6 * CH), BF16),
            pltpu.VMEM((6 * CH, LAT), BF16),
            pltpu.VMEM((LAT, CH), BF16),
            pltpu.VMEM((LAT, LAT), F32),
            pltpu.VMEM((8, EDGES), F32),
            pltpu.VMEM((16, EDGES), F32),
            pltpu.VMEM((NSLOT, 8, ATOMS), F32),
            pltpu.VMEM((NSLOT, 8, ATOMS), F32),
            dma((NSLOT,)),
            dma((NSLOT,)),
            dma((13,)),
            dma((13,)),
            dma((NSLOT,)),
            dma((NSLOT,)),
        ],
        compiler_params=pltpu.CompilerParams(collective_id=0, has_side_effects=True),
    )(
        positions.reshape(3, ATOMS),
        features.reshape(ROWS, ATOMS),
        species.reshape(1, ATOMS),
        edges.reshape(2, EDGES),
        edge_count.reshape(1, 1),
        emb_table,
        w_first,
        w_second,
        w_out.reshape(1, CH),
    )
    return (forces.reshape(1, 1, 1, 3, ATOMS), energy.reshape(1, 1, 1, EDGES))


def solution(mesh):
    placed = (
        P("plate", "tower", "gz", None, None),
        P("plate", "tower", "gz", None, None),
        P("plate", "tower", "gz", None),
        P(),
        P("plate", "tower", "gz", None, None),
        P("plate", "tower", "gz"),
        P(),
        P(),
        P(),
    )
    return jax.shard_map(
        shards,
        mesh=mesh,
        in_specs=placed,
        out_specs=(P("plate", "tower", "gz", None, None), P("plate", "tower", "gz", None)),
        check_vma=False,
    )
```

time: 106 us -> 54.9 us (0.52)
  the two profiles are of different devices: /device:TPU:6 before, /device:TPU:2 now
where the time goes in v1:
time: 54.9 us; the launch traced here: 54.6 us
  Pallas kernels  48.6 us (89%)
  local copies, waits for them, and re-layouts  4.76 us (9%)
  between operations  1.3 us (2%)
    pallas_call x1, Pallas kernels, shards(): pl.pallas_call(kernel, name='edge_forces', out_shape=(jax.ShapeDtypeStruc...  48.6 us
    unnamed x10, local copies, waits for them, and re-layouts  4.76 us

profile of v1, /device:TPU:2, one launch (start us, length us, event | category | flops | bytes accessed | tf_op | source)
XLA Modules:
  0.0 54.6 jit_solution(13356327743759402914)
XLA Ops:
  1.3 0.0 copy-start.2
  1.3 0.7 %copy-done.2 = f32[1,1,1,3,128]{4,2,3,1,0:T(1,128)S(1)} copy-done((f32[1,1,1,3,128]{4,2,3,1,0:T(1,128)S(1)}, f32[1,1,1,3,128]{4,2,3,1,0:T(1,128)}, u32[]{:S(2)}) %copy-start.2) | copy-done | bytes 1560
  2.0 0.6 %copy.15 = f32[1,1,1,3,128]{4,3,2,1,0:T(4,128)} copy(f32[1,1,1,3,128]{4,2,3,1,0:T(1,128)S(1)} %copy-done.2) | data formatting | bytes 3072
  2.5 1.6 %copy.11.w1_ref = bf16[128,328]{1,0:T(8,128)(2,1)} copy(bf16[128,328]{0,1:T(8,128)(2,1)} %param.15) | data formatting | bytes 167936 | tf_op args[6]
  4.2 48.6 %edge_forces.1 = (f32[3,128]{1,0:T(4,128)}, f32[1,512]{1,0:T(1,128)}) custom-call(f32[3,128]{1,0:T(4,128)} %bitcast.12, bf16[576,128]{1,0:T(8,128)(2,1)} %bitcast.11, s32[1,128]{1,0:T(1,128)} %bitcast.16, s32[2,512]{1,0:T(2,128)} %bitcast.13, s32[1,1]{1,0:T(1,128)} %bitcast.10.count_ref, bf16[6,64]{1,0:T(8,128)(2,1)} %table_ref.1, ...), custom_call_target="tpu_custom_call" | custom-call | tf_op jit(solution)/shard_map/edge_forces/pallas_call | solution.py:315
  52.7 0.0 copy-start
  52.7 0.6 %copy-done = f32[3,128]{1,0:T(4,128)S(1)} copy-done((f32[3,128]{1,0:T(4,128)S(1)}, f32[3,128]{1,0:T(4,128)}, u32[]{:S(2)}) %copy-start) | copy-done | bytes 1560
  53.4 0.0 copy-start.1
  53.4 0.6 %copy.12 = f32[1,1,1,3,128]{4,2,3,1,0:T(1,128)} copy(f32[1,1,1,3,128]{4,3,2,1,0:T(4,128)S(1)} %bitcast.14) | data formatting | bytes 3072
  53.9 0.1 copy-done.1
  54.1 0.6 %copy.18 = f32[1,1,1,512]{3,2,1,0:T(1,128)} copy(f32[1,1,1,512]{3,2,1,0:T(1,128)S(1)} %bitcast.15) | data formatting | bytes 4096
Async XLA Ops:
  1.3 0.7 %copy-start.2 = (f32[1,1,1,3,128]{4,2,3,1,0:T(1,128)S(1)}, f32[1,1,1,3,128]{4,2,3,1,0:T(1,128)}, u32[]{:S(2)}) copy-start(f32[1,1,1,3,128]{4,2,3,1,0:T(1,128)} %param.9) | copy-start | bytes 4612
  52.7 0.7 %copy-start = (f32[3,128]{1,0:T(4,128)S(1)}, f32[3,128]{1,0:T(4,128)}, u32[]{:S(2)}) copy-start(f32[3,128]{1,0:T(4,128)} %get-tuple-element.4) | copy-start | bytes 4612
  53.4 0.7 %copy-start.1 = (f32[1,512]{1,0:T(1,128)S(1)}, f32[1,512]{1,0:T(1,128)}, u32[]{:S(2)}) copy-start(f32[1,512]{1,0:T(1,128)} %get-tuple-element.5) | copy-start | bytes 6148

commit v2 on v1

--- a/solution.py
+++ b/solution.py
@@ -45,8 +45,75 @@
     return sign * s * x, sign * c_
 
 
+def remote(src, dst, ssem, rsem, to):
+    return pltpu.make_async_remote_copy(
+        src_ref=src,
+        dst_ref=dst,
+        send_sem=ssem,
+        recv_sem=rsem,
+        device_id=to,
+        device_id_type=pl.DeviceIdType.MESH,
+    )
+
+
+def fetch(pairs, sems):
+    copies = [pltpu.make_async_copy(src, dst, sems.at[n]) for n, (src, dst) in enumerate(pairs)]
+    for c in copies:
+        c.start()
+    return copies
+
+
+def pack_small(pos, spec, stage, out):
+    stage[...] = jnp.zeros_like(stage)
+    for k in range(3):
+        hi = pos[k].astype(BF16).astype(F32)
+        stage[k : k + 1, :] = hi
+        stage[k + 3 : k + 4, :] = (pos[k] - hi).astype(BF16).astype(F32)
+    stage[6:7, :] = spec[...].astype(F32)
+    out[...] = stage[...].astype(BF16)
+
+
+DEPTH = 16
+
+
+def early_kernel(pos_any, feat_any, spec_any, sib_feat, sib_meta, pos, spec, stage, mown, lsem, ssem, rsem):
+    n_plate = lax.axis_size("plate")
+    p, t, g = (lax.axis_index(a) for a in ("plate", "tower", "gz"))
+    sibling = {"plate": lax.rem(p + DEPTH, n_plate), "tower": t, "gz": g}
+
+    @pl.when(lax.rem(p, DEPTH) == 0)
+    def _():
+        barrier = pltpu.get_barrier_semaphore()
+        pl.semaphore_signal(barrier, inc=1, device_id=sibling, device_id_type=pl.DeviceIdType.MESH)
+        for c in fetch([(pos_any, pos), (spec_any, spec)], lsem):
+            c.wait()
+        pack_small(pos, spec, stage, mown)
+        pl.semaphore_wait(barrier, 1)
+        copies = [
+            remote(feat_any, sib_feat, ssem.at[0], rsem.at[0], sibling),
+            remote(mown, sib_meta, ssem.at[1], rsem.at[1], sibling),
+        ]
+        for c in copies:
+            c.start()
+        for c in copies:
+            c.wait()
+
+
 def kernel(
-    pos_ref,
+    pos_any,
+    feat_any,
+    spec_any,
+    edges_any,
+    count_any,
+    table_any,
+    w1_any,
+    w2_any,
+    wout_any,
+    sib_feat,
+    sib_meta,
+    force_ref,
+    energy_ref,
+    pos,
     feat_ref,
     spec_ref,
     edges_ref,
@@ -55,8 +122,9 @@
     w1_ref,
     w2_ref,
     wout_ref,
-    force_ref,
-    energy_ref,
+    sib_f,
+    sib_m,
+    relay,
     fslot,
     mown,
     mslot,
@@ -74,9 +142,11 @@
     w2t,
     tmat,
     gbuf,
-    rad,
+    stage,
     pout,
     pslot,
+    lsem,
+    xsem,
     msend,
     mrecv,
     fsend,
@@ -91,6 +161,9 @@
     outward = lax.rem(t + 2 * odd - 1 + n_tower, n_tower)
     g_up, g_dn = lax.rem(g + 1, n_gz), lax.rem(g + n_gz - 1, n_gz)
     p_up, p_dn = lax.rem(p + 1, n_plate), lax.rem(p + n_plate - 1, n_plate)
+    z = lax.rem(p, DEPTH)
+    last = z // (DEPTH - 1)
+    first = lax.rem(z + DEPTH - 1, DEPTH) // (DEPTH - 1)
 
     def dev(pp, tt, gg):
         return {"plate": pp, "tower": tt, "gz": gg}
@@ -101,31 +174,43 @@
         dev(p_up, t, g), dev(p_dn, t, g),
     ]
     home = [dest[k] for k in (1, 0, 2, 3, 5, 4, 7, 6, 9, 8)]
+    sibling = dev(lax.rem(p + DEPTH, n_plate), t, g)
+    below = dev(lax.rem(p + n_plate - 1 + DEPTH * first, n_plate), t, g)
+    above = dev(lax.rem(p + 1 + DEPTH * last, n_plate), t, g)
 
     barrier = pltpu.get_barrier_semaphore()
-    for d in dest:
+
+    def greet(d):
         pl.semaphore_signal(barrier, inc=1, device_id=d, device_id_type=pl.DeviceIdType.MESH)
 
-    pos = pos_ref[...]
-    hi = pos.astype(BF16).astype(F32)
-    lo = (pos - hi).astype(BF16).astype(F32)
-    rad[...] = jnp.zeros_like(rad)
-    rad[0:3, 0:ATOMS] = hi
-    rad[3:6, 0:ATOMS] = lo
-    rad[6:7, 0:ATOMS] = spec_ref[...].astype(F32)
-    mown[...] = rad[:, 0:ATOMS].astype(BF16)
-
-    def remote(src, dst, ssem, rsem, to):
-        return pltpu.make_async_remote_copy(
-            src_ref=src,
-            dst_ref=dst,
-            send_sem=ssem,
-            recv_sem=rsem,
-            device_id=to,
-            device_id_type=pl.DeviceIdType.MESH,
-        )
-
-    meta = [remote(mown, mslot.at[k], msend.at[k], mrecv.at[k], dest[k]) for k in range(NSLOT)]
+    for d in (below, above, *dest[:8]):
+        greet(d)
+
+    @pl.when(z == 0)
+    def _():
+        greet(dest[9])
+        greet(sibling)
+
+    small = fetch([(pos_any, pos), (spec_any, spec_ref)], lsem)
+    rest = fetch(
+        [
+            (feat_any, feat_ref), (edges_any, edges_ref), (count_any, count_ref), (table_any, table_ref),
+            (w1_any, w1_ref), (w2_any, w2_ref), (wout_any, wout_ref),
+        ],
+        xsem,
+    )
+    for c in small:
+        c.wait()
+    pack_small(pos, spec_ref, stage, mown)
+
+    @pl.when(z == 0)
+    def _():
+        for c in fetch([(sib_feat, sib_f), (sib_meta, sib_m)], lsem):
+            c.wait()
+
+    meta = [remote(mown, mslot.at[k], msend.at[k], mrecv.at[k], dest[k]) for k in range(NSLOT - 1)]
+    meta.append(remote(mown, mslot.at[9], msend.at[9], mrecv.at[9], below))
+    meta_sib = remote(sib_m, mslot.at[9], msend.at[9], mrecv.at[9], below)
     top, low = pl.ds(0, HALF), pl.ds(HALF, HALF)
 
     def feature(n, src, slot, to, part=None):
@@ -138,17 +223,45 @@
     f_g_dn = feature(1, feat_ref, 1, dest[1])
     f_part = feature(2, feat_ref, 2, dest[2])
     f_out = [feature(3, feat_ref, 3, dest[3], top), feature(4, feat_ref, 3, dest[3], low)]
-    f_p_up = feature(5, feat_ref, 8, dest[8])
-    f_p_dn = feature(6, feat_ref, 9, dest[9])
+    f_p_dn = feature(6, feat_ref, 9, below)
+    f_p_sib = feature(6, sib_f, 9, below)
+    f_p_up = feature(5, feat_ref, 8, dest[8], top)
+    f_p_low = feature(13, feat_ref, 8, above, low)
+    f_p_via = remote(feat_ref.at[low], relay, fsend.at[13], frecv.at[14], above)
+    r_up_low = remote(relay, fslot.at[8].at[low], fsend.at[14], frecv.at[13], sibling)
     r_part = [feature(7, fslot.at[0], 4, dest[2]), feature(8, fslot.at[1], 5, dest[2])]
     r_up = [feature(9, fslot.at[3], 6, dest[0], top), feature(10, fslot.at[3], 6, dest[0], low)]
     r_dn = [feature(11, fslot.at[3], 7, dest[1], top), feature(12, fslot.at[3], 7, dest[1], low)]
 
-    pl.semaphore_wait(barrier, NSLOT)
-    for c in meta:
+    rest[0].wait()
+    pl.semaphore_wait(barrier, NSLOT + first + last)
+    for c in meta[:9]:
         c.start()
-    for c in (f_out[0], f_out[1], f_g_up, f_g_dn, f_p_up, f_p_dn, f_part):
+
+    @pl.when(z == 0)
+    def _():
+        meta_sib.start()
+        f_p_sib.start()
+
+    @pl.when(z != 0)
+    def _():
+        meta[9].start()
+        f_p_dn.start()
+
+    f_p_up.start()
+
+    @pl.when(last == 1)
+    def _():
+        f_p_via.start()
+
+    @pl.when(last != 1)
+    def _():
+        f_p_low.start()
+
+    for c in (f_out[0], f_out[1], f_g_up, f_g_dn, f_part):
         c.start()
+    for c in rest[1:]:
+        c.wait()
 
     left, right = edges_ref[0:1, :], edges_ref[1:2, :]
     row = lax.broadcasted_iota(jnp.int32, (3 * ATOMS, EDGES), 0)
@@ -163,11 +276,12 @@
     turned = jnp.transpose(tmat[...])
     embt = turned[0:CH, :].astype(BF16)
     wout = turned[0:CH, 6:7]
-    wtmp[...] = jnp.zeros_like(wtmp)
-    wtmp[:, 0 : RB + 5 * CH] = w1_ref[...].astype(F32)
-    wfull = pltpu.roll(wtmp[...], 6 * CH - RB, 1)
-    wp[...] = wfull.astype(BF16)
-    wpt[...] = jnp.transpose(wfull).astype(BF16)
+    wtmp[0 : 5 * CH, :] = w1_ref[RB : RB + 5 * CH, :].astype(F32)
+    wtmp[5 * CH : 6 * CH - RB, :] = jnp.zeros((CH - RB, LAT), F32)
+    wtmp[6 * CH - RB : 6 * CH, :] = w1_ref[0:RB, :].astype(F32)
+    wfull = wtmp[...]
+    wpt[...] = wfull.astype(BF16)
+    wp[...] = jnp.transpose(wfull).astype(BF16)
     w2t[...] = jnp.transpose(w2_ref[...].astype(F32)).astype(BF16)
 
     f_out[0].wait_recv()
@@ -180,6 +294,11 @@
     r_part[0].start()
     f_g_dn.wait_recv()
     r_part[1].start()
+
+    @pl.when(z == 0)
+    def _():
+        f_p_via.wait_recv()
+        r_up_low.start()
 
     for c in meta:
         c.wait_recv()
@@ -223,8 +342,9 @@
         c.wait_recv()
     order = [fslot[0], feat_ref[...], fslot[1], fslot[4], fslot[2], fslot[5], fslot[6], fslot[3], fslot[7]]
     gj[...] = dot(jnp.concatenate(order, 1), ohc[...])
+    f_p_dn.wait_recv()
     f_p_up.wait_recv()
-    f_p_dn.wait_recv()
+    f_p_low.wait_recv()
     gi[...] = dot(jnp.concatenate([fslot[8], feat_ref[...], fslot[9]], 1), ohp[...])
 
     def rows_of(ref, m, k):
@@ -299,26 +419,65 @@
     for c in back:
         c.start()
     total = lanes(part_p, 1) + lanes(part_c, 1)
-    for c in (*meta, f_g_up, f_g_dn, f_part, *f_out, f_p_up, f_p_dn, *r_part, *r_up, *r_dn):
+    for c in (*meta, f_g_up, f_g_dn, f_part, *f_out, f_p_up, f_p_low, f_p_dn, *r_part, *r_up, *r_dn):
         c.wait_send()
+
+    @pl.when(z == 0)
+    def _():
+        r_up_low.wait_send()
+
     for k, c in enumerate(back):
         c.wait_recv()
         total = total + pslot[k]
-    force_ref[...] = total[0:3, :]
+    for k in range(3):
+        force_ref[k] = total[k : k + 1, :]
     for c in back:
         c.wait_send()
 
 
 def shards(positions, features, species, emb_table, edges, edge_count, w_first, w_second, w_out):
     vmem = pl.BlockSpec(memory_space=pltpu.VMEM)
+    hbm = pl.BlockSpec(memory_space=pl.ANY)
     dma = pltpu.SemaphoreType.DMA
+    pos = jnp.transpose(positions.reshape(1, 3, ATOMS), (1, 0, 2))
+    feat = features.reshape(ROWS, ATOMS)
+    spec = species.reshape(1, ATOMS)
+    small = [pltpu.VMEM((3, 1, ATOMS), F32), pltpu.VMEM((1, ATOMS), jnp.int32)]
+    sib_feat, sib_meta = pl.pallas_call(
+        early_kernel,
+        name="early_exchange",
+        out_shape=(jax.ShapeDtypeStruct((ROWS, ATOMS), BF16), jax.ShapeDtypeStruct((16, ATOMS), BF16)),
+        in_specs=[hbm] * 3,
+        out_specs=(hbm, hbm),
+        scratch_shapes=[
+            *small,
+            pltpu.VMEM((16, ATOMS), F32),
+            pltpu.VMEM((16, ATOMS), BF16),
+            dma((2,)),
+            dma((2,)),
+            dma((2,)),
+        ],
+        compiler_params=pltpu.CompilerParams(collective_id=1, has_side_effects=True),
+    )(pos, feat, spec)
     forces, energy = pl.pallas_call(
         kernel,
         name="edge_forces",
-        out_shape=(jax.ShapeDtypeStruct((3, ATOMS), F32), jax.ShapeDtypeStruct((1, EDGES), F32)),
-        in_specs=[vmem, vmem, vmem, vmem, pl.BlockSpec(memory_space=pltpu.SMEM), vmem, vmem, vmem, vmem],
+        out_shape=(jax.ShapeDtypeStruct((3, 1, ATOMS), F32), jax.ShapeDtypeStruct((1, EDGES), F32)),
+        in_specs=[hbm] * 11,
         out_specs=(vmem, vmem),
         scratch_shapes=[
+            small[0],
+            pltpu.VMEM((ROWS, ATOMS), BF16),
+            small[1],
+            pltpu.VMEM((2, EDGES), jnp.int32),
+            pltpu.SMEM((1, 1), jnp.int32),
+            pltpu.VMEM((6, CH), BF16),
+            pltpu.VMEM((RB + 5 * CH, LAT), BF16),
+            pltpu.VMEM((CH, LAT), BF16),
+            pltpu.VMEM((1, CH), BF16),
+            pltpu.VMEM((ROWS, ATOMS), BF16),
+            pltpu.VMEM((16, ATOMS), BF16),
+            pltpu.VMEM((HALF, ATOMS), BF16),
             pltpu.VMEM((NSLOT, ROWS, ATOMS), BF16),
             pltpu.VMEM((16, ATOMS), BF16),
             pltpu.VMEM((NSLOT, 16, ATOMS), BF16),
@@ -330,35 +489,42 @@
             pltpu.VMEM((3 * CH, EDGES), F32),
             pltpu.VMEM((8, 8, EDGES), F32),
             pltpu.VMEM((6 * CH, EDGES), BF16),
-            pltpu.VMEM((LAT, 6 * CH), F32),
+            pltpu.VMEM((6 * CH, LAT), F32),
             pltpu.VMEM((LAT, 6 * CH), BF16),
             pltpu.VMEM((6 * CH, LAT), BF16),
             pltpu.VMEM((LAT, CH), BF16),
             pltpu.VMEM((LAT, LAT), F32),
             pltpu.VMEM((8, EDGES), F32),
-            pltpu.VMEM((16, EDGES), F32),
+            pltpu.VMEM((16, ATOMS), F32),
             pltpu.VMEM((NSLOT, 8, ATOMS), F32),
             pltpu.VMEM((NSLOT, 8, ATOMS), F32),
+            dma((2,)),
+            dma((7,)),
             dma((NSLOT,)),
             dma((NSLOT,)),
-            dma((13,)),
-            dma((13,)),
+            dma((15,)),
+            dma((15,)),
             dma((NSLOT,)),
             dma((NSLOT,)),
         ],
         compiler_params=pltpu.CompilerParams(collective_id=0, has_side_effects=True),
     )(
-        positions.reshape(3, ATOMS),
-        features.reshape(ROWS, ATOMS),
-        species.reshape(1, ATOMS),
+        pos,
+        feat,
+        spec,
         edges.reshape(2, EDGES),
         edge_count.reshape(1, 1),
         emb_table,
-        w_first,
+        w_first.T,
         w_second,
         w_out.reshape(1, CH),
-    )
-    return (forces.reshape(1, 1, 1, 3, ATOMS), energy.reshape(1, 1, 1, EDGES))
+        sib_feat,
+        sib_meta,
+    )
+    return (
+        jnp.transpose(forces, (1, 0, 2)).reshape(1, 1, 1, 3, ATOMS),
+        energy.reshape(1, 1, 1, EDGES),
+    )
 
 
 def solution(mesh):

time: 54.9 us -> 49.5 us (0.902)
  local copies, waits for them, and re-layouts: 4.76 us -> 1.76 us
  Pallas kernels: 48.6 us -> 46.2 us
    pallas_call x1, Pallas kernels: 48.6 us -> 32.3 us  [shards(): pl.pallas_call(kernel, name='edge_forces', out_shape=(jax.ShapeDtypeStruc...]
    pallas_call x0 -> x1, Pallas kernels: none -> 13.9 us  [shards(): pl.pallas_call(early_kernel, name='early_exchange', out_shape=(jax.ShapeD...]
    unnamed x10 -> x6, local copies, waits for them, and re-layouts: 4.76 us -> 1.76 us
where the time goes in v2:
time: 49.5 us; the launch traced here: 49.3 us
  Pallas kernels  46.2 us (93%)
  local copies, waits for them, and re-layouts  1.76 us (4%)
  between operations  1.31 us (3%)
    pallas_call x1, Pallas kernels, shards(): pl.pallas_call(kernel, name='edge_forces', out_shape=(jax.ShapeDtypeStruc...  32.3 us
    pallas_call x1, Pallas kernels, shards(): pl.pallas_call(early_kernel, name='early_exchange', out_shape=(jax.ShapeD...  13.9 us
    unnamed x6, local copies, waits for them, and re-layouts  1.76 us

profile of v2, /device:TPU:2, one launch (start us, length us, event | category | flops | bytes accessed | tf_op | source)
XLA Modules:
  0.0 49.3 jit_solution(15027362444216603504)
XLA Ops:
  1.3 13.9 %early_exchange.1 = (bf16[576,128]{1,0:T(8,128)(2,1)}, bf16[16,128]{1,0:T(8,128)(2,1)}) custom-call(f32[3,1,128]{2,1,0:T(1,128)} %bitcast.15, bf16[576,128]{1,0:T(8,128)(2,1)} %bitcast.12, s32[1,128]{1,0:T(1,128)} %bitcast.18), custom_call_target="tpu_custom_call" | custom-call | tf_op jit(solution)/shard_map/early_exchange/pallas_call | solution.py:446
  15.2 32.3 %edge_forces.1 = (f32[3,1,128]{2,1,0:T(1,128)}, f32[1,512]{1,0:T(1,128)}) custom-call(f32[3,1,128]{2,1,0:T(1,128)} %bitcast.16, bf16[576,128]{1,0:T(8,128)(2,1)} %bitcast.13, s32[1,128]{1,0:T(1,128)} %bitcast.19, s32[2,512]{1,0:T(2,128)} %bitcast.17, s32[1,1]{1,0:T(1,128)} %bitcast.11.count_any, bf16[6,64]{1,0:T(8,128)(2,1)} %table_any.1, ...), custom_call_target="tpu_custom_call" | custom-call | tf_op jit(solution)/shard_map/edge_forces/pallas_call | solution.py:462
  47.5 0.0 copy-start.1
  47.5 0.0 copy-start
  47.5 0.6 %copy-done.1 = f32[3,1,128]{2,1,0:T(1,128)S(1)} copy-done((f32[3,1,128]{2,1,0:T(1,128)S(1)}, f32[3,1,128]{2,1,0:T(1,128)}, u32[]{:S(2)}) %copy-start.1) | copy-done | bytes 1560
  48.1 0.6 %copy.15 = f32[1,1,1,3,128]{4,2,3,1,0:T(1,128)} copy(f32[1,1,1,3,128]{4,2,3,1,0:T(1,128)S(1)} %bitcast.21) | data formatting | bytes 3072
  48.7 0.0 copy-done
  48.7 0.6 %copy.16 = f32[1,1,1,512]{3,2,1,0:T(1,128)} copy(f32[1,1,1,512]{3,2,1,0:T(1,128)S(1)} %bitcast.20) | data formatting | bytes 4096
Async XLA Ops:
  47.5 0.6 %copy-start.1 = (f32[3,1,128]{2,1,0:T(1,128)S(1)}, f32[3,1,128]{2,1,0:T(1,128)}, u32[]{:S(2)}) copy-start(f32[3,1,128]{2,1,0:T(1,128)} %get-tuple-element.8) | copy-start | bytes 4612
  47.5 1.2 %copy-start = (f32[1,512]{1,0:T(1,128)S(1)}, f32[1,512]{1,0:T(1,128)}, u32[]{:S(2)}) copy-start(f32[1,512]{1,0:T(1,128)} %get-tuple-element.9) | copy-start | bytes 6148

commit v3 on v2

--- a/solution.py
+++ b/solution.py
@@ -76,29 +76,6 @@
 DEPTH = 16
 
 
-def early_kernel(pos_any, feat_any, spec_any, sib_feat, sib_meta, pos, spec, stage, mown, lsem, ssem, rsem):
-    n_plate = lax.axis_size("plate")
-    p, t, g = (lax.axis_index(a) for a in ("plate", "tower", "gz"))
-    sibling = {"plate": lax.rem(p + DEPTH, n_plate), "tower": t, "gz": g}
-
-    @pl.when(lax.rem(p, DEPTH) == 0)
-    def _():
-        barrier = pltpu.get_barrier_semaphore()
-        pl.semaphore_signal(barrier, inc=1, device_id=sibling, device_id_type=pl.DeviceIdType.MESH)
-        for c in fetch([(pos_any, pos), (spec_any, spec)], lsem):
-            c.wait()
-        pack_small(pos, spec, stage, mown)
-        pl.semaphore_wait(barrier, 1)
-        copies = [
-            remote(feat_any, sib_feat, ssem.at[0], rsem.at[0], sibling),
-            remote(mown, sib_meta, ssem.at[1], rsem.at[1], sibling),
-        ]
-        for c in copies:
-            c.start()
-        for c in copies:
-            c.wait()
-
-
 def kernel(
     pos_any,
     feat_any,
@@ -109,8 +86,6 @@
     w1_any,
     w2_any,
     wout_any,
-    sib_feat,
-    sib_meta,
     force_ref,
     energy_ref,
     pos,
@@ -124,7 +99,6 @@
     wout_ref,
     sib_f,
     sib_m,
-    relay,
     fslot,
     mown,
     mslot,
@@ -146,7 +120,7 @@
     pout,
     pslot,
     lsem,
-    xsem,
+    ready,
     msend,
     mrecv,
     fsend,
@@ -176,14 +150,14 @@
     home = [dest[k] for k in (1, 0, 2, 3, 5, 4, 7, 6, 9, 8)]
     sibling = dev(lax.rem(p + DEPTH, n_plate), t, g)
     below = dev(lax.rem(p + n_plate - 1 + DEPTH * first, n_plate), t, g)
-    above = dev(lax.rem(p + 1 + DEPTH * last, n_plate), t, g)
+    above = dev(lax.rem(p + 1 + DEPTH, n_plate), t, g)
 
     barrier = pltpu.get_barrier_semaphore()
 
     def greet(d):
         pl.semaphore_signal(barrier, inc=1, device_id=d, device_id_type=pl.DeviceIdType.MESH)
 
-    for d in (below, above, *dest[:8]):
+    for d in (below, *dest[:8]):
         greet(d)
 
     @pl.when(z == 0)
@@ -191,22 +165,21 @@
         greet(dest[9])
         greet(sibling)
 
-    small = fetch([(pos_any, pos), (spec_any, spec_ref)], lsem)
-    rest = fetch(
+    @pl.when(last == 0)
+    def _():
+        greet(dest[8])
+
+    small = fetch(
         [
-            (feat_any, feat_ref), (edges_any, edges_ref), (count_any, count_ref), (table_any, table_ref),
-            (w1_any, w1_ref), (w2_any, w2_ref), (wout_any, wout_ref),
+            (pos_any, pos), (spec_any, spec_ref), (feat_any, feat_ref), (edges_any, edges_ref), (count_any, count_ref),
+            (table_any, table_ref), (w1_any, w1_ref), (w2_any, w2_ref), (wout_any, wout_ref),
         ],
-        xsem,
-    )
+        lsem,
+    )
+    small, rest = small[:2], small[2:]
     for c in small:
         c.wait()
     pack_small(pos, spec_ref, stage, mown)
-
-    @pl.when(z == 0)
-    def _():
-        for c in fetch([(sib_feat, sib_f), (sib_meta, sib_m)], lsem):
-            c.wait()
 
     meta = [remote(mown, mslot.at[k], msend.at[k], mrecv.at[k], dest[k]) for k in range(NSLOT - 1)]
     meta.append(remote(mown, mslot.at[9], msend.at[9], mrecv.at[9], below))
@@ -225,41 +198,37 @@
     f_out = [feature(3, feat_ref, 3, dest[3], top), feature(4, feat_ref, 3, dest[3], low)]
     f_p_dn = feature(6, feat_ref, 9, below)
     f_p_sib = feature(6, sib_f, 9, below)
-    f_p_up = feature(5, feat_ref, 8, dest[8], top)
-    f_p_low = feature(13, feat_ref, 8, above, low)
-    f_p_via = remote(feat_ref.at[low], relay, fsend.at[13], frecv.at[14], above)
-    r_up_low = remote(relay, fslot.at[8].at[low], fsend.at[14], frecv.at[13], sibling)
+    f_p_up = feature(5, feat_ref, 8, dest[8])
+    sib_feat = remote(feat_ref, sib_f, fsend.at[13], frecv.at[13], sibling)
+    sib_meta = remote(mown, sib_m, fsend.at[14], frecv.at[14], sibling)
     r_part = [feature(7, fslot.at[0], 4, dest[2]), feature(8, fslot.at[1], 5, dest[2])]
     r_up = [feature(9, fslot.at[3], 6, dest[0], top), feature(10, fslot.at[3], 6, dest[0], low)]
     r_dn = [feature(11, fslot.at[3], 7, dest[1], top), feature(12, fslot.at[3], 7, dest[1], low)]
 
     rest[0].wait()
-    pl.semaphore_wait(barrier, NSLOT + first + last)
+    pl.semaphore_wait(barrier, NSLOT + last)
+
+    @pl.when(last == 1)
+    def _():
+        pl.semaphore_signal(ready, inc=1, device_id=above, device_id_type=pl.DeviceIdType.MESH)
+
+    @pl.when(z == 0)
+    def _():
+        sib_meta.start()
+        sib_feat.start()
+
     for c in meta[:9]:
         c.start()
-
-    @pl.when(z == 0)
-    def _():
-        meta_sib.start()
-        f_p_sib.start()
+    f_p_up.start()
 
     @pl.when(z != 0)
     def _():
         meta[9].start()
         f_p_dn.start()
 
-    f_p_up.start()
-
-    @pl.when(last == 1)
-    def _():
-        f_p_via.start()
-
-    @pl.when(last != 1)
-    def _():
-        f_p_low.start()
-
     for c in (f_out[0], f_out[1], f_g_up, f_g_dn, f_part):
         c.start()
+
     for c in rest[1:]:
         c.wait()
 
@@ -297,8 +266,11 @@
 
     @pl.when(z == 0)
     def _():
-        f_p_via.wait_recv()
-        r_up_low.start()
+        sib_meta.wait_recv()
+        sib_feat.wait_recv()
+        pl.semaphore_wait(ready, 1)
+        meta_sib.start()
+        f_p_sib.start()
 
     for c in meta:
         c.wait_recv()
@@ -344,7 +316,6 @@
     gj[...] = dot(jnp.concatenate(order, 1), ohc[...])
     f_p_dn.wait_recv()
     f_p_up.wait_recv()
-    f_p_low.wait_recv()
     gi[...] = dot(jnp.concatenate([fslot[8], feat_ref[...], fslot[9]], 1), ohp[...])
 
     def rows_of(ref, m, k):
@@ -419,12 +390,13 @@
     for c in back:
         c.start()
     total = lanes(part_p, 1) + lanes(part_c, 1)
-    for c in (*meta, f_g_up, f_g_dn, f_part, *f_out, f_p_up, f_p_low, f_p_dn, *r_part, *r_up, *r_dn):
+    for c in (*meta, f_g_up, f_g_dn, f_part, *f_out, f_p_up, f_p_dn, *r_part, *r_up, *r_dn):
         c.wait_send()
 
     @pl.when(z == 0)
     def _():
-        r_up_low.wait_send()
+        sib_meta.wait_send()
+        sib_feat.wait_send()
 
     for k, c in enumerate(back):
         c.wait_recv()
@@ -443,27 +415,11 @@
     feat = features.reshape(ROWS, ATOMS)
     spec = species.reshape(1, ATOMS)
     small = [pltpu.VMEM((3, 1, ATOMS), F32), pltpu.VMEM((1, ATOMS), jnp.int32)]
-    sib_feat, sib_meta = pl.pallas_call(
-        early_kernel,
-        name="early_exchange",
-        out_shape=(jax.ShapeDtypeStruct((ROWS, ATOMS), BF16), jax.ShapeDtypeStruct((16, ATOMS), BF16)),
-        in_specs=[hbm] * 3,
-        out_specs=(hbm, hbm),
-        scratch_shapes=[
-            *small,
-            pltpu.VMEM((16, ATOMS), F32),
-            pltpu.VMEM((16, ATOMS), BF16),
-            dma((2,)),
-            dma((2,)),
-            dma((2,)),
-        ],
-        compiler_params=pltpu.CompilerParams(collective_id=1, has_side_effects=True),
-    )(pos, feat, spec)
     forces, energy = pl.pallas_call(
         kernel,
         name="edge_forces",
-        out_shape=(jax.ShapeDtypeStruct((3, 1, ATOMS), F32), jax.ShapeDtypeStruct((1, EDGES), F32)),
-        in_specs=[hbm] * 11,
+        out_shape=(pltpu.VMEM((3, 1, ATOMS), F32), pltpu.VMEM((1, EDGES), F32)),
+        in_specs=[hbm] * 9,
         out_specs=(vmem, vmem),
         scratch_shapes=[
             small[0],
@@ -477,7 +433,6 @@
             pltpu.VMEM((1, CH), BF16),
             pltpu.VMEM((ROWS, ATOMS), BF16),
             pltpu.VMEM((16, ATOMS), BF16),
-            pltpu.VMEM((HALF, ATOMS), BF16),
             pltpu.VMEM((NSLOT, ROWS, ATOMS), BF16),
             pltpu.VMEM((16, ATOMS), BF16),
             pltpu.VMEM((NSLOT, 16, ATOMS), BF16),
@@ -498,8 +453,8 @@
             pltpu.VMEM((16, ATOMS), F32),
             pltpu.VMEM((NSLOT, 8, ATOMS), F32),
             pltpu.VMEM((NSLOT, 8, ATOMS), F32),
-            dma((2,)),
-            dma((7,)),
+            dma((9,)),
+            pltpu.SemaphoreType.REGULAR,
             dma((NSLOT,)),
             dma((NSLOT,)),
             dma((15,)),
@@ -518,8 +473,6 @@
         w_first.T,
         w_second,
         w_out.reshape(1, CH),
-        sib_feat,
-        sib_meta,
     )
     return (
         jnp.transpose(forces, (1, 0, 2)).reshape(1, 1, 1, 3, ATOMS),

time: 49.5 us -> 45.3 us (0.915)
  the two profiles are of different devices: /device:TPU:2 before, /device:TPU:1 now
where the time goes in v3:
time: 45.3 us; the launch traced here: 45 us
  Pallas kernels  42.5 us (94%)
  between operations  1.29 us (3%)
  local copies, waits for them, and re-layouts  1.14 us (3%)
    pallas_call x1, Pallas kernels, shards(): pl.pallas_call(kernel, name='edge_forces', out_shape=(pltpu.VMEM((3, 1, A...  42.5 us
    unnamed x2, local copies, waits for them, and re-layouts  1.14 us

profile of v3, /device:TPU:1, one launch (start us, length us, event | category | flops | bytes accessed | tf_op | source)
XLA Modules:
  0.0 45.0 jit_solution(1560026230423366477)
XLA Ops:
  1.3 42.5 %edge_forces.1 = (f32[3,1,128]{2,1,0:T(1,128)S(1)}, f32[1,512]{1,0:T(1,128)S(1)}) custom-call(f32[3,1,128]{2,1,0:T(1,128)} %bitcast.17, bf16[576,128]{1,0:T(8,128)(2,1)} %bitcast.14, s32[1,128]{1,0:T(1,128)} %bitcast.18, s32[2,512]{1,0:T(2,128)} %bitcast.16, s32[1,1]{1,0:T(1,128)} %bitcast.11.count_any, bf16[6,64]{1,0:T(8,128)(2,1)} %table_any.1, ...), custom_call_target="tpu_custom_call" | custom-call | tf_op jit(solution)/shard_map/edge_forces/pallas_call | solution.py:418
  43.8 0.6 %copy.14 = f32[1,1,1,3,128]{4,2,3,1,0:T(1,128)} copy(f32[1,1,1,3,128]{4,2,3,1,0:T(1,128)S(1)} %bitcast.13) | data formatting | bytes 3072
  44.4 0.6 %copy.15 = f32[1,1,1,512]{3,2,1,0:T(1,128)} copy(f32[1,1,1,512]{3,2,1,0:T(1,128)S(1)} %bitcast.12) | data formatting | bytes 4096

commit v4 on v3

--- a/solution.py
+++ b/solution.py
@@ -121,6 +121,7 @@
     pslot,
     lsem,
     ready,
+    go,
     msend,
     mrecv,
     fsend,
@@ -139,8 +140,14 @@
     last = z // (DEPTH - 1)
     first = lax.rem(z + DEPTH - 1, DEPTH) // (DEPTH - 1)
 
+    total = n_plate * n_tower * n_gz
+
     def dev(pp, tt, gg):
         return {"plate": pp, "tower": tt, "gz": gg}
+
+    def is_late(d):
+        return 1 - ((d["plate"] * n_tower + d["tower"]) * n_gz + d["gz"] + total - 1) // total
+
 
     dest = [
         dev(p, t, g_up), dev(p, t, g_dn), dev(p, partner, g), dev(p, outward, g),
@@ -157,12 +164,24 @@
     def greet(d):
         pl.semaphore_signal(barrier, inc=1, device_id=d, device_id_type=pl.DeviceIdType.MESH)
 
-    for d in (below, *dest[:8]):
-        greet(d)
+    late = is_late(dev(p, t, g))
+    late_to = [is_late(d) for d in dest[:4]]
+    late_sib = first * is_late(sibling)
+    near = late_to[0] + late_to[1] + late_to[2] + late_to[3] + late_sib
+
+    greet(below)
+
+    @pl.when(late == 0)
+    def _():
+        for d in dest[:4]:
+            greet(d)
 
     @pl.when(z == 0)
     def _():
         greet(dest[9])
+
+    @pl.when(first - late == 1)
+    def _():
         greet(sibling)
 
     @pl.when(last == 0)
@@ -181,8 +200,13 @@
         c.wait()
     pack_small(pos, spec_ref, stage, mown)
 
-    meta = [remote(mown, mslot.at[k], msend.at[k], mrecv.at[k], dest[k]) for k in range(NSLOT - 1)]
-    meta.append(remote(mown, mslot.at[9], msend.at[9], mrecv.at[9], below))
+    def small_rows(src, k, to):
+        return remote(src, mslot.at[k], msend.at[k], mrecv.at[k], to)
+
+    meta = [small_rows(mown, k, dest[k]) for k in range(4)]
+    m_part = [small_rows(mslot.at[k], 4 + k, dest[2]) for k in range(2)]
+    m_up, m_dn = small_rows(mslot.at[3], 6, dest[0]), small_rows(mslot.at[3], 7, dest[1])
+    meta += [*m_part, m_up, m_dn, small_rows(mown, 8, dest[8]), small_rows(mown, 9, below)]
     meta_sib = remote(sib_m, mslot.at[9], msend.at[9], mrecv.at[9], below)
     top, low = pl.ds(0, HALF), pl.ds(HALF, HALF)
 
@@ -206,19 +230,27 @@
     r_dn = [feature(11, fslot.at[3], 7, dest[1], top), feature(12, fslot.at[3], 7, dest[1], low)]
 
     rest[0].wait()
-    pl.semaphore_wait(barrier, NSLOT + last)
+    pl.semaphore_wait(barrier, 6 + last - near)
+
+    def tell(sem, d):
+        pl.semaphore_signal(sem, inc=1, device_id=d, device_id_type=pl.DeviceIdType.MESH)
 
     @pl.when(last == 1)
     def _():
-        pl.semaphore_signal(ready, inc=1, device_id=above, device_id_type=pl.DeviceIdType.MESH)
-
-    @pl.when(z == 0)
+        tell(ready, above)
+
+    @pl.when(late == 1)
+    def _():
+        for d in (*dest[:4], sibling):
+            tell(go, d)
+
+    @pl.when(first - late_sib == 1)
     def _():
         sib_meta.start()
         sib_feat.start()
 
-    for c in meta[:9]:
-        c.start()
+    direct = ((meta[0], f_g_up), (meta[1], f_g_dn), (meta[2], f_part), (meta[3], *f_out))
+    meta[8].start()
     f_p_up.start()
 
     @pl.when(z != 0)
@@ -226,8 +258,12 @@
         meta[9].start()
         f_p_dn.start()
 
-    for c in (f_out[0], f_out[1], f_g_up, f_g_dn, f_part):
-        c.start()
+    for k in (3, 0, 1, 2):
+
+        @pl.when(late_to[k] == 0)
+        def _(k=k):
+            for c in direct[k]:
+                c.start()
 
     for c in rest[1:]:
         c.wait()
@@ -253,16 +289,36 @@
     wp[...] = jnp.transpose(wfull).astype(BF16)
     w2t[...] = jnp.transpose(w2_ref[...].astype(F32)).astype(BF16)
 
+    @pl.when(near == 1)
+    def _():
+        pl.semaphore_wait(go, 1)
+
+        @pl.when(late_sib == 1)
+        def _():
+            sib_meta.start()
+            sib_feat.start()
+
+        for k in (3, 0, 1, 2):
+
+            @pl.when(late_to[k] == 1)
+            def _(k=k):
+                for c in direct[k]:
+                    c.start()
+
+    meta[3].wait_recv()
+    m_up.start()
+    m_dn.start()
     f_out[0].wait_recv()
     r_up[0].start()
     r_dn[0].start()
     f_out[1].wait_recv()
     r_up[1].start()
     r_dn[1].start()
-    f_g_up.wait_recv()
-    r_part[0].start()
-    f_g_dn.wait_recv()
-    r_part[1].start()
+    for k, c in enumerate((f_g_up, f_g_dn)):
+        meta[k].wait_recv()
+        m_part[k].start()
+        c.wait_recv()
+        r_part[k].start()
 
     @pl.when(z == 0)
     def _():
@@ -272,7 +328,7 @@
         meta_sib.start()
         f_p_sib.start()
 
-    for c in meta:
+    for c in (meta[2], *meta[8:], m_up, m_dn, *m_part):
         c.wait_recv()
     mi = dot(jnp.concatenate([mslot[8], mown[...], mslot[9]], 1), ohp[...])
     order = [mslot[0], mown[...], mslot[1], mslot[4], mslot[2], mslot[5], mslot[6], mslot[3], mslot[7]]
@@ -389,7 +445,7 @@
     back = [remote(pout.at[k], pslot.at[k], psend.at[k], precv.at[k], home[k]) for k in range(NSLOT)]
     for c in back:
         c.start()
-    total = lanes(part_p, 1) + lanes(part_c, 1)
+    force = lanes(part_p, 1) + lanes(part_c, 1)
     for c in (*meta, f_g_up, f_g_dn, f_part, *f_out, f_p_up, f_p_dn, *r_part, *r_up, *r_dn):
         c.wait_send()
 
@@ -400,9 +456,9 @@
 
     for k, c in enumerate(back):
         c.wait_recv()
-        total = total + pslot[k]
+        force = force + pslot[k]
     for k in range(3):
-        force_ref[k] = total[k : k + 1, :]
+        force_ref[k] = force[k : k + 1, :]
     for c in back:
         c.wait_send()
 
@@ -455,6 +511,7 @@
             pltpu.VMEM((NSLOT, 8, ATOMS), F32),
             dma((9,)),
             pltpu.SemaphoreType.REGULAR,
+            pltpu.SemaphoreType.REGULAR,
             dma((NSLOT,)),
             dma((NSLOT,)),
             dma((15,)),

time: 45.3 us -> 41.6 us (0.918)
  Pallas kernels: 42.5 us -> 38.4 us
    pallas_call x1, Pallas kernels: 42.5 us -> 38.4 us  [shards(): pl.pallas_call(kernel, name='edge_forces', out_shape=(pltpu.VMEM((3, 1, A...]
where the time goes in v4:
time: 41.6 us; the launch traced here: 40.8 us
  Pallas kernels  38.4 us (92%)
  between operations  1.29 us (3%)
  local copies, waits for them, and re-layouts  1.14 us (3%)
    pallas_call x1, Pallas kernels, shards(): pl.pallas_call(kernel, name='edge_forces', out_shape=(pltpu.VMEM((3, 1, A...  38.4 us
    unnamed x2, local copies, waits for them, and re-layouts  1.14 us

profile of v4, /device:TPU:1, one launch (start us, length us, event | category | flops | bytes accessed | tf_op | source)
XLA Modules:
  0.0 40.8 jit_solution(14292023316474927858)
XLA Ops:
  1.3 38.4 %edge_forces.1 = (f32[3,1,128]{2,1,0:T(1,128)S(1)}, f32[1,512]{1,0:T(1,128)S(1)}) custom-call(f32[3,1,128]{2,1,0:T(1,128)} %bitcast.17, bf16[576,128]{1,0:T(8,128)(2,1)} %bitcast.14, s32[1,128]{1,0:T(1,128)} %bitcast.18, s32[2,512]{1,0:T(2,128)} %bitcast.16, s32[1,1]{1,0:T(1,128)} %bitcast.11.count_any, bf16[6,64]{1,0:T(8,128)(2,1)} %table_any.1, ...), custom_call_target="tpu_custom_call" | custom-call | tf_op jit(solution)/shard_map/edge_forces/pallas_call | solution.py:474
  39.7 0.6 %copy.14 = f32[1,1,1,3,128]{4,2,3,1,0:T(1,128)} copy(f32[1,1,1,3,128]{4,2,3,1,0:T(1,128)S(1)} %bitcast.13) | data formatting | bytes 3072
  40.2 0.6 %copy.15 = f32[1,1,1,512]{3,2,1,0:T(1,128)} copy(f32[1,1,1,512]{3,2,1,0:T(1,128)S(1)} %bitcast.12) | data formatting | bytes 4096

commit v5 on v4

--- a/solution.py
+++ b/solution.py
@@ -24,10 +24,6 @@
 
 def dot(a, b):
     return lax.dot_general(a, b, (((1,), (0,)), ((), ())), preferred_element_type=F32)
-
-
-def dot_nt(a, b):
-    return lax.dot_general(a, b, (((1,), (1,)), ((), ())), preferred_element_type=F32)
 
 
 def sin_cos_pi(t):
@@ -104,6 +100,8 @@
     mslot,
     ohp,
     ohc,
+    ohpt,
+    ohct,
     gi,
     gj,
     si,
@@ -269,11 +267,28 @@
         c.wait()
 
     left, right = edges_ref[0:1, :], edges_ref[1:2, :]
-    row = lax.broadcasted_iota(jnp.int32, (3 * ATOMS, EDGES), 0)
-    ohp[...] = jnp.where(row == left, 1.0, 0.0).astype(BF16)
-    for k, u in enumerate((1, 2 - 2 * odd, 2 * odd)):
-        shifted = right - 3 * ATOMS * u
-        ohc[3 * ATOMS * k : 3 * ATOMS * (k + 1), :] = jnp.where(row == shifted, 1.0, 0.0).astype(BF16)
+    row = lax.broadcasted_iota(jnp.int32, (ATOMS, EDGES), 0)
+    lane = lax.broadcasted_iota(jnp.int32, (EDGES, ATOMS), 1)
+
+    def column_of(index):
+        turned = jnp.transpose(jnp.broadcast_to(index.astype(F32), (8, EDGES)))
+        return jnp.broadcast_to(turned[:, 0:1].astype(jnp.int32), (EDGES, ATOMS))
+
+    left_col, right_col = column_of(left), column_of(right)
+
+    def one_hot(match):
+        return jnp.where(match, 1.0, 0.0).astype(BF16)
+
+    for k in range(3):
+        base = ATOMS * k
+        ohp[base : base + ATOMS, :] = one_hot(row == left - base)
+        ohpt[:, base : base + ATOMS] = one_hot(lane == left_col - base)
+    u_part, u_out = 2 - 2 * odd, 2 * odd
+    places = ((1, 0), (1, 1), (1, 2), (u_part, 1), (u_out, 1), (u_part, 0), (u_part, 2), (u_out, 0), (u_out, 2))
+    for k, (u, v) in enumerate(places):
+        base = (3 * u + v) * ATOMS
+        ohc[ATOMS * k : ATOMS * (k + 1), :] = one_hot(row == right - base)
+        ohct[:, ATOMS * k : ATOMS * (k + 1)] = one_hot(lane == right_col - base)
 
     tmat[...] = jnp.zeros_like(tmat)
     tmat[0:6, 0:CH] = table_ref[...].astype(F32)
@@ -331,7 +346,7 @@
     for c in (meta[2], *meta[8:], m_up, m_dn, *m_part):
         c.wait_recv()
     mi = dot(jnp.concatenate([mslot[8], mown[...], mslot[9]], 1), ohp[...])
-    order = [mslot[0], mown[...], mslot[1], mslot[4], mslot[2], mslot[5], mslot[6], mslot[3], mslot[7]]
+    order = [mslot[0], mown[...], *(mslot[k] for k in range(1, 8))]
     mj = dot(jnp.concatenate(order, 1), ohc[...])
     off_i = jnp.where(left < ATOMS, -1.0, jnp.where(left < 2 * ATOMS, 0.0, 1.0))
     off_u = jnp.where(right < 3 * ATOMS, 0, jnp.where(right < 6 * ATOMS, 1, 2))
@@ -365,36 +380,59 @@
     xbuf[5 * CH : 6 * CH - 16, :] = jnp.zeros((CH - 16, EDGES), BF16)
     xbuf[6 * CH - 16 : 6 * CH, :] = jnp.concatenate([jnp.zeros_like(radial), radial], 0).astype(BF16)
 
-    f_part.wait_recv()
-    for c in (*r_part, *r_up, *r_dn):
-        c.wait_recv()
-    order = [fslot[0], feat_ref[...], fslot[1], fslot[4], fslot[2], fslot[5], fslot[6], fslot[3], fslot[7]]
-    gj[...] = dot(jnp.concatenate(order, 1), ohc[...])
-    f_p_dn.wait_recv()
-    f_p_up.wait_recv()
-    gi[...] = dot(jnp.concatenate([fslot[8], feat_ref[...], fslot[9]], 1), ohp[...])
-
     def rows_of(ref, m, k):
         return ref[m * CH + 8 * k : m * CH + 8 * k + 8, :]
 
-    for k2 in range(CH // 16):
-        prods = [[], [], []]
-        for k in (2 * k2, 2 * k2 + 1):
-            sums = []
-            for ref in (gi, gj):
+    def degree_sums(ref, out, other=None):
+        for k2 in range(CH // 16):
+            prods = [[], [], []]
+            for k in (2 * k2, 2 * k2 + 1):
                 one = [rows_of(ref, m, k) * yb[m - 1] for m in range(1, 9)]
-                sums.append((
+                sums = (
                     rows_of(ref, 0, k),
                     one[0] + one[1] + one[2],
                     one[3] + one[4] + one[5] + one[6] + one[7],
-                ))
-            for l in range(3):
-                si[l * CH + 8 * k : l * CH + 8 * k + 8, :] = sums[0][l]
-                sj[l * CH + 8 * k : l * CH + 8 * k + 8, :] = sums[1][l]
-                prods[l].append(sums[0][l] * sums[1][l])
-        for l in range(3):
-            start = (2 + l) * CH + 16 * k2
-            xbuf[start : start + 16, :] = jnp.concatenate(prods[l], 0).astype(BF16)
+                )
+                for l in range(3):
+                    at = slice(l * CH + 8 * k, l * CH + 8 * k + 8)
+                    out[at, :] = sums[l]
+                    if other is not None:
+                        prods[l].append(sums[l] * other[at, :])
+            if other is not None:
+                for l in range(3):
+                    start = (2 + l) * CH + 16 * k2
+                    xbuf[start : start + 16, :] = jnp.concatenate(prods[l], 0).astype(BF16)
+
+    def last_columns():
+        for c in (*r_up, *r_dn):
+            c.wait_recv()
+        gj[...] = gj[...] + dot(jnp.concatenate([fslot[6], fslot[7]], 1), ohc[7 * ATOMS :, :])
+
+    f_part.wait_recv()
+    for c in r_part:
+        c.wait_recv()
+    order = [fslot[0], feat_ref[...], *(fslot[k] for k in range(1, 6))]
+    gj[...] = dot(jnp.concatenate(order, 1), ohc[0 : 7 * ATOMS, :])
+
+    @pl.when(z == 0)
+    def _():
+        f_p_dn.wait_recv()
+        gi[...] = dot(jnp.concatenate([feat_ref[...], fslot[9]], 1), ohp[ATOMS:, :])
+        last_columns()
+        degree_sums(gj, sj)
+        f_p_up.wait_recv()
+        gi[...] = gi[...] + dot(fslot[8], ohp[0:ATOMS, :])
+        degree_sums(gi, si, sj)
+
+    @pl.when(z != 0)
+    def _():
+        f_p_dn.wait_recv()
+        f_p_up.wait_recv()
+        gi[...] = dot(jnp.concatenate([fslot[8], feat_ref[...], fslot[9]], 1), ohp[...])
+        degree_sums(gi, si)
+        last_columns()
+        degree_sums(gj, sj, si)
+
     z1 = dot(wp[...], xbuf[...])
     sig1 = 1.0 / (1.0 + jnp.exp(-z1))
     z2 = dot(w2_ref[...], (z1 * sig1).astype(BF16))
@@ -430,21 +468,22 @@
     grad = gbuf[...]
     g_hi = grad.astype(BF16).astype(F32)
     both = jnp.concatenate([g_hi, grad - g_hi], 0).astype(BF16)
-    part_p = dot_nt(both, ohp[...])
-    part_p = part_p[0:8] + part_p[8:16]
-    part_c = dot_nt(both, ohc[...])
-    part_c = -(part_c[0:8] + part_c[8:16])
 
     def lanes(a, k):
         return a[:, k * ATOMS : (k + 1) * ATOMS]
 
-    for slot, k in enumerate((0, 2, 4, 7, 3, 5, 6, 8)):
-        pout[slot] = lanes(part_c, k)
+    back = [remote(pout.at[k], pslot.at[k], psend.at[k], precv.at[k], home[k]) for k in range(NSLOT)]
+    part_p = dot(both, ohpt[...])
+    part_p = part_p[0:8] + part_p[8:16]
     pout[8] = lanes(part_p, 0)
     pout[9] = lanes(part_p, 2)
-    back = [remote(pout.at[k], pslot.at[k], psend.at[k], precv.at[k], home[k]) for k in range(NSLOT)]
-    for c in back:
-        c.start()
+    back[8].start()
+    back[9].start()
+    part_c = dot(both, ohct[...])
+    part_c = -(part_c[0:8] + part_c[8:16])
+    for slot, k in enumerate((0, 2, 3, 4, 5, 6, 7, 8)):
+        pout[slot] = lanes(part_c, k)
+        back[slot].start()
     force = lanes(part_p, 1) + lanes(part_c, 1)
     for c in (*meta, f_g_up, f_g_dn, f_part, *f_out, f_p_up, f_p_dn, *r_part, *r_up, *r_dn):
         c.wait_send()
@@ -461,6 +500,12 @@
         force_ref[k] = force[k : k + 1, :]
     for c in back:
         c.wait_send()
+
+
+def finish(force_ref, energy_ref, force_out, energy_out, sems):
+    copies = fetch([(force_ref, force_out), (energy_ref, energy_out)], sems)
+    for c in copies:
+        c.wait()
 
 
 def shards(positions, features, species, emb_table, edges, edge_count, w_first, w_second, w_out):
@@ -494,6 +539,8 @@
             pltpu.VMEM((NSLOT, 16, ATOMS), BF16),
             pltpu.VMEM((3 * ATOMS, EDGES), BF16),
             pltpu.VMEM((9 * ATOMS, EDGES), BF16),
+            pltpu.VMEM((EDGES, 3 * ATOMS), BF16),
+            pltpu.VMEM((EDGES, 9 * ATOMS), BF16),
             pltpu.VMEM((ROWS, EDGES), F32),
             pltpu.VMEM((ROWS, EDGES), F32),
             pltpu.VMEM((3 * CH, EDGES), F32),
@@ -531,6 +578,17 @@
         w_second,
         w_out.reshape(1, CH),
     )
+    forces, energy = pl.pallas_call(
+        finish,
+        name="finish",
+        out_shape=(jax.ShapeDtypeStruct((3, 1, ATOMS), F32), jax.ShapeDtypeStruct((1, EDGES), F32)),
+        in_specs=[vmem, vmem],
+        out_specs=(hbm, hbm),
+        scratch_shapes=[dma((2,))],
+    )(
+        pltpu.with_memory_space_constraint(forces, pltpu.VMEM),
+        pltpu.with_memory_space_constraint(energy, pltpu.VMEM),
+    )
     return (
         jnp.transpose(forces, (1, 0, 2)).reshape(1, 1, 1, 3, ATOMS),
         energy.reshape(1, 1, 1, EDGES),

time: 41.6 us -> 40.2 us (0.966); the launches traced: 40.8 us -> 40 us
  local copies, waits for them, and re-layouts: 1.14 us -> 0 us
    unnamed x2 -> x0, local copies, waits for them, and re-layouts: 1.14 us -> none
    pallas_call x0 -> x1, Pallas kernels: none -> 0.6 us  [shards(): pl.pallas_call(finish, name='finish', out_shape=(jax.ShapeDtypeStruct((3,...]
where the time goes in v5:
time: 40.2 us; the launch traced here: 40 us
  Pallas kernels  38.7 us (96%)
  between operations  1.29 us (3%)
    pallas_call x1, Pallas kernels, shards(): pl.pallas_call(kernel, name='edge_forces', out_shape=(pltpu.VMEM((3, 1, A...  38.1 us

profile of v5, /device:TPU:1, one launch (start us, length us, event | category | flops | bytes accessed | tf_op | source)
XLA Modules:
  0.0 40.0 jit_solution(5024810340470098182)
XLA Ops:
  1.3 38.1 %edge_forces.1 = (f32[3,1,128]{2,1,0:T(1,128)S(1)}, f32[1,512]{1,0:T(1,128)S(1)}) custom-call(f32[3,1,128]{2,1,0:T(1,128)} %bitcast.15, bf16[576,128]{1,0:T(8,128)(2,1)} %bitcast.12, s32[1,128]{1,0:T(1,128)} %bitcast.16, s32[2,512]{1,0:T(2,128)} %bitcast.14, s32[1,1]{1,0:T(1,128)} %bitcast.11.count_any, bf16[6,64]{1,0:T(8,128)(2,1)} %table_any.1, ...), custom_call_target="tpu_custom_call" | custom-call | tf_op jit(solution)/shard_map/edge_forces/pallas_call | solution.py:519
  39.4 0.6 %finish.1 = (f32[3,1,128]{2,1,0:T(1,128)}, f32[1,512]{1,0:T(1,128)}) custom-call(f32[3,1,128]{2,1,0:T(1,128)S(1)} %get-tuple-element.6.force_ref, f32[1,512]{1,0:T(1,128)S(1)} %get-tuple-element.7.energy_ref), custom_call_target="tpu_custom_call" | custom-call | tf_op jit(solution)/shard_map/finish/pallas_call | solution.py:581

commit v6 on v5

--- a/solution.py
+++ b/solution.py
@@ -13,7 +13,7 @@
 LAT = 128
 RB = 8
 ROWS = 9 * CH
-HALF = ROWS // 2
+PART = ROWS // 4
 RADIUS = 3.0
 SOFTEN = 0.04
 F32 = jnp.float32
@@ -77,7 +77,7 @@
     feat_any,
     spec_any,
     edges_any,
-    count_any,
+    count_ref,
     table_any,
     w1_any,
     w2_any,
@@ -88,7 +88,6 @@
     feat_ref,
     spec_ref,
     edges_ref,
-    count_ref,
     table_ref,
     w1_ref,
     w2_ref,
@@ -124,6 +123,8 @@
     mrecv,
     fsend,
     frecv,
+    ssend,
+    srecv,
     psend,
     precv,
 ):
@@ -157,6 +158,13 @@
     below = dev(lax.rem(p + n_plate - 1 + DEPTH * first, n_plate), t, g)
     above = dev(lax.rem(p + 1 + DEPTH, n_plate), t, g)
 
+    loads = fetch(
+        [
+            (feat_any, feat_ref), (pos_any, pos), (spec_any, spec_ref), (edges_any, edges_ref),
+            (table_any, table_ref), (w1_any, w1_ref), (w2_any, w2_ref), (wout_any, wout_ref),
+        ],
+        lsem,
+    )
     barrier = pltpu.get_barrier_semaphore()
 
     def greet(d):
@@ -167,6 +175,8 @@
     late_sib = first * is_late(sibling)
     near = late_to[0] + late_to[1] + late_to[2] + late_to[3] + late_sib
 
+    via_lo = last * (1 - p // DEPTH)
+
     greet(below)
 
     @pl.when(late == 0)
@@ -186,48 +196,51 @@
     def _():
         greet(dest[8])
 
-    small = fetch(
-        [
-            (pos_any, pos), (spec_any, spec_ref), (feat_any, feat_ref), (edges_any, edges_ref), (count_any, count_ref),
-            (table_any, table_ref), (w1_any, w1_ref), (w2_any, w2_ref), (wout_any, wout_ref),
-        ],
-        lsem,
-    )
-    small, rest = small[:2], small[2:]
-    for c in small:
+    for c in loads[1:3]:
         c.wait()
     pack_small(pos, spec_ref, stage, mown)
 
     def small_rows(src, k, to):
-        return remote(src, mslot.at[k], msend.at[k], mrecv.at[k], to)
+        n = {0: 0, 1: 1, 3: 2}.get(k, 3)
+        return remote(src, mslot.at[k], msend, mrecv.at[n], to)
 
     meta = [small_rows(mown, k, dest[k]) for k in range(4)]
     m_part = [small_rows(mslot.at[k], 4 + k, dest[2]) for k in range(2)]
     m_up, m_dn = small_rows(mslot.at[3], 6, dest[0]), small_rows(mslot.at[3], 7, dest[1])
-    meta += [*m_part, m_up, m_dn, small_rows(mown, 8, dest[8]), small_rows(mown, 9, below)]
-    meta_sib = remote(sib_m, mslot.at[9], msend.at[9], mrecv.at[9], below)
-    top, low = pl.ds(0, HALF), pl.ds(HALF, HALF)
+    meta += [small_rows(mown, 8, dest[8]), small_rows(mown, 9, below)]
+    meta_sib = small_rows(sib_m, 9, below)
+    def of_size(ref, ssem, rsem):
+        return remote(ref, ref, ssem, rsem, dest[0])
+
+    parts = [pl.ds(PART * k, PART) for k in range(ROWS // PART)]
 
     def feature(n, src, slot, to, part=None):
         dst = fslot.at[slot]
         if part is not None:
             src, dst = src.at[part], dst.at[part]
-        return remote(src, dst, fsend.at[n], frecv.at[n], to)
+        return remote(src, dst, fsend, frecv.at[n], to)
 
     f_g_up = feature(0, feat_ref, 0, dest[0])
     f_g_dn = feature(1, feat_ref, 1, dest[1])
     f_part = feature(2, feat_ref, 2, dest[2])
-    f_out = [feature(3, feat_ref, 3, dest[3], top), feature(4, feat_ref, 3, dest[3], low)]
-    f_p_dn = feature(6, feat_ref, 9, below)
-    f_p_sib = feature(6, sib_f, 9, below)
-    f_p_up = feature(5, feat_ref, 8, dest[8])
-    sib_feat = remote(feat_ref, sib_f, fsend.at[13], frecv.at[13], sibling)
-    sib_meta = remote(mown, sib_m, fsend.at[14], frecv.at[14], sibling)
-    r_part = [feature(7, fslot.at[0], 4, dest[2]), feature(8, fslot.at[1], 5, dest[2])]
-    r_up = [feature(9, fslot.at[3], 6, dest[0], top), feature(10, fslot.at[3], 6, dest[0], low)]
-    r_dn = [feature(11, fslot.at[3], 7, dest[1], top), feature(12, fslot.at[3], 7, dest[1], low)]
-
-    rest[0].wait()
+    r_part = [feature(2, fslot.at[0], 4, dest[2]), feature(2, fslot.at[1], 5, dest[2])]
+    r_up = [feature(3, fslot.at[3], 6, dest[0], c) for c in parts]
+    r_dn = [feature(3, fslot.at[3], 7, dest[1], c) for c in parts]
+    f_p_up = [feature(4, feat_ref, 8, dest[8], pl.ds(ROWS // 2 * k, ROWS // 2)) for k in range(2)]
+    up_all = of_size(fslot.at[8], fsend, frecv.at[4])
+    f_p_dn = feature(5, feat_ref, 9, below)
+    f_p_sib = feature(5, sib_f, 9, below)
+    f_out = [feature(6 + k, feat_ref, 3, dest[3], c) for k, c in enumerate(parts)]
+    sib_feat = remote(feat_ref, sib_f, ssend.at[0], srecv.at[0], sibling)
+    sib_meta = remote(mown, sib_m, ssend.at[1], srecv.at[1], sibling)
+
+    meta_sent, feat_sent = of_size(mslot, msend, msend), of_size(fslot, fsend, fsend)
+    meta_rest = of_size(mslot.at[pl.ds(3, 7)], msend, mrecv.at[3])
+    near_come = of_size(fslot.at[pl.ds(4, 3)], fsend, frecv.at[2])
+    far_come = of_size(fslot.at[pl.ds(6, 2)], fsend, frecv.at[3])
+    back_all = of_size(pslot, psend, precv)
+
+    loads[0].wait()
     pl.semaphore_wait(barrier, 6 + last - near)
 
     def tell(sem, d):
@@ -248,12 +261,16 @@
         sib_feat.start()
 
     direct = ((meta[0], f_g_up), (meta[1], f_g_dn), (meta[2], f_part), (meta[3], *f_out))
-    meta[8].start()
-    f_p_up.start()
+    meta[4].start()
+    f_p_up[0].start()
+
+    @pl.when(via_lo == 0)
+    def _():
+        f_p_up[1].start()
 
     @pl.when(z != 0)
     def _():
-        meta[9].start()
+        meta[5].start()
         f_p_dn.start()
 
     for k in (3, 0, 1, 2):
@@ -263,7 +280,7 @@
             for c in direct[k]:
                 c.start()
 
-    for c in rest[1:]:
+    for c in loads[3:]:
         c.wait()
 
     left, right = edges_ref[0:1, :], edges_ref[1:2, :]
@@ -323,12 +340,14 @@
     meta[3].wait_recv()
     m_up.start()
     m_dn.start()
-    f_out[0].wait_recv()
-    r_up[0].start()
-    r_dn[0].start()
-    f_out[1].wait_recv()
-    r_up[1].start()
-    r_dn[1].start()
+    for k, c in enumerate(f_out):
+        c.wait_recv()
+        r_up[k].start()
+        r_dn[k].start()
+    @pl.when(via_lo == 1)
+    def _():
+        f_p_up[1].start()
+
     for k, c in enumerate((f_g_up, f_g_dn)):
         meta[k].wait_recv()
         m_part[k].start()
@@ -343,8 +362,7 @@
         meta_sib.start()
         f_p_sib.start()
 
-    for c in (meta[2], *meta[8:], m_up, m_dn, *m_part):
-        c.wait_recv()
+    meta_rest.wait_recv()
     mi = dot(jnp.concatenate([mslot[8], mown[...], mslot[9]], 1), ohp[...])
     order = [mslot[0], mown[...], *(mslot[k] for k in range(1, 8))]
     mj = dot(jnp.concatenate(order, 1), ohc[...])
@@ -404,13 +422,10 @@
                     xbuf[start : start + 16, :] = jnp.concatenate(prods[l], 0).astype(BF16)
 
     def last_columns():
-        for c in (*r_up, *r_dn):
-            c.wait_recv()
+        far_come.wait_recv()
         gj[...] = gj[...] + dot(jnp.concatenate([fslot[6], fslot[7]], 1), ohc[7 * ATOMS :, :])
 
-    f_part.wait_recv()
-    for c in r_part:
-        c.wait_recv()
+    near_come.wait_recv()
     order = [fslot[0], feat_ref[...], *(fslot[k] for k in range(1, 6))]
     gj[...] = dot(jnp.concatenate(order, 1), ohc[0 : 7 * ATOMS, :])
 
@@ -420,14 +435,14 @@
         gi[...] = dot(jnp.concatenate([feat_ref[...], fslot[9]], 1), ohp[ATOMS:, :])
         last_columns()
         degree_sums(gj, sj)
-        f_p_up.wait_recv()
+        up_all.wait_recv()
         gi[...] = gi[...] + dot(fslot[8], ohp[0:ATOMS, :])
         degree_sums(gi, si, sj)
 
     @pl.when(z != 0)
     def _():
         f_p_dn.wait_recv()
-        f_p_up.wait_recv()
+        up_all.wait_recv()
         gi[...] = dot(jnp.concatenate([fslot[8], feat_ref[...], fslot[9]], 1), ohp[...])
         degree_sums(gi, si)
         last_columns()
@@ -472,7 +487,7 @@
     def lanes(a, k):
         return a[:, k * ATOMS : (k + 1) * ATOMS]
 
-    back = [remote(pout.at[k], pslot.at[k], psend.at[k], precv.at[k], home[k]) for k in range(NSLOT)]
+    back = [remote(pout.at[k], pslot.at[k], psend, precv, home[k]) for k in range(NSLOT)]
     part_p = dot(both, ohpt[...])
     part_p = part_p[0:8] + part_p[8:16]
     pout[8] = lanes(part_p, 0)
@@ -485,21 +500,20 @@
         pout[slot] = lanes(part_c, k)
         back[slot].start()
     force = lanes(part_p, 1) + lanes(part_c, 1)
-    for c in (*meta, f_g_up, f_g_dn, f_part, *f_out, f_p_up, f_p_dn, *r_part, *r_up, *r_dn):
-        c.wait_send()
-
-    @pl.when(z == 0)
+    meta_sent.wait_send()
+    feat_sent.wait_send()
+
+    @pl.when(first == 1)
     def _():
         sib_meta.wait_send()
         sib_feat.wait_send()
 
-    for k, c in enumerate(back):
-        c.wait_recv()
+    back_all.wait_recv()
+    for k in range(NSLOT):
         force = force + pslot[k]
     for k in range(3):
         force_ref[k] = force[k : k + 1, :]
-    for c in back:
-        c.wait_send()
+    back_all.wait_send()
 
 
 def finish(force_ref, energy_ref, force_out, energy_out, sems):
@@ -520,14 +534,13 @@
         kernel,
         name="edge_forces",
         out_shape=(pltpu.VMEM((3, 1, ATOMS), F32), pltpu.VMEM((1, EDGES), F32)),
-        in_specs=[hbm] * 9,
+        in_specs=[*[hbm] * 4, pl.BlockSpec(memory_space=pltpu.SMEM), *[hbm] * 4],
         out_specs=(vmem, vmem),
         scratch_shapes=[
             small[0],
             pltpu.VMEM((ROWS, ATOMS), BF16),
             small[1],
             pltpu.VMEM((2, EDGES), jnp.int32),
-            pltpu.SMEM((1, 1), jnp.int32),
             pltpu.VMEM((6, CH), BF16),
             pltpu.VMEM((RB + 5 * CH, LAT), BF16),
             pltpu.VMEM((CH, LAT), BF16),
@@ -556,15 +569,17 @@
             pltpu.VMEM((16, ATOMS), F32),
             pltpu.VMEM((NSLOT, 8, ATOMS), F32),
             pltpu.VMEM((NSLOT, 8, ATOMS), F32),
-            dma((9,)),
+            dma((8,)),
             pltpu.SemaphoreType.REGULAR,
             pltpu.SemaphoreType.REGULAR,
-            dma((NSLOT,)),
-            dma((NSLOT,)),
-            dma((15,)),
-            dma((15,)),
-            dma((NSLOT,)),
-            dma((NSLOT,)),
+            dma,
+            dma((4,)),
+            dma,
+            dma((6 + ROWS // PART,)),
+            dma((2,)),
+            dma((2,)),
+            dma,
+            dma,
         ],
         compiler_params=pltpu.CompilerParams(collective_id=0, has_side_effects=True),
     )(

time: 40.2 us -> 39.6 us (0.985)
  Pallas kernels: 38.7 us -> 38.1 us
    pallas_call x1, Pallas kernels: 38.1 us -> 37.5 us  [shards(): pl.pallas_call(kernel, name='edge_forces', out_shape=(pltpu.VMEM((3, 1, A...]
where the time goes in v6:
time: 39.6 us; the launch traced here: 39.4 us
  Pallas kernels  38.1 us (96%)
  between operations  1.29 us (3%)
    pallas_call x1, Pallas kernels, shards(): pl.pallas_call(kernel, name='edge_forces', out_shape=(pltpu.VMEM((3, 1, A...  37.5 us

profile of v6, /device:TPU:1, one launch (start us, length us, event | category | flops | bytes accessed | tf_op | source)
XLA Modules:
  0.0 39.4 jit_solution(14771263936116979220)
XLA Ops:
  1.3 37.5 %edge_forces.1 = (f32[3,1,128]{2,1,0:T(1,128)S(1)}, f32[1,512]{1,0:T(1,128)S(1)}) custom-call(f32[3,1,128]{2,1,0:T(1,128)} %bitcast.15, bf16[576,128]{1,0:T(8,128)(2,1)} %bitcast.12, s32[1,128]{1,0:T(1,128)} %bitcast.16, s32[2,512]{1,0:T(2,128)} %bitcast.14, s32[1,1]{1,0:T(1,128)} %bitcast.11.count_ref, bf16[6,64]{1,0:T(8,128)(2,1)} %table_any.1, ...), custom_call_target="tpu_custom_call" | custom-call | tf_op jit(solution)/shard_map/edge_forces/pallas_call | solution.py:533
  38.8 0.6 %finish.1 = (f32[3,1,128]{2,1,0:T(1,128)}, f32[1,512]{1,0:T(1,128)}) custom-call(f32[3,1,128]{2,1,0:T(1,128)S(1)} %get-tuple-element.6.force_ref, f32[1,512]{1,0:T(1,128)S(1)} %get-tuple-element.7.energy_ref), custom_call_target="tpu_custom_call" | custom-call | tf_op jit(solution)/shard_map/finish/pallas_call | solution.py:596

commit v7 on v6

--- a/solution.py
+++ b/solution.py
@@ -52,8 +52,8 @@
     )
 
 
-def fetch(pairs, sems):
-    copies = [pltpu.make_async_copy(src, dst, sems.at[n]) for n, (src, dst) in enumerate(pairs)]
+def fetch(pairs, sems, base=0):
+    copies = [pltpu.make_async_copy(src, dst, sems.at[base + n]) for n, (src, dst) in enumerate(pairs)]
     for c in copies:
         c.start()
     return copies
@@ -77,7 +77,7 @@
     feat_any,
     spec_any,
     edges_any,
-    count_ref,
+    count_any,
     table_any,
     w1_any,
     w2_any,
@@ -88,6 +88,7 @@
     feat_ref,
     spec_ref,
     edges_ref,
+    count_ref,
     table_ref,
     w1_ref,
     w2_ref,
@@ -158,13 +159,7 @@
     below = dev(lax.rem(p + n_plate - 1 + DEPTH * first, n_plate), t, g)
     above = dev(lax.rem(p + 1 + DEPTH, n_plate), t, g)
 
-    loads = fetch(
-        [
-            (feat_any, feat_ref), (pos_any, pos), (spec_any, spec_ref), (edges_any, edges_ref),
-            (table_any, table_ref), (w1_any, w1_ref), (w2_any, w2_ref), (wout_any, wout_ref),
-        ],
-        lsem,
-    )
+    loads = fetch([(feat_any, feat_ref)], lsem)
     barrier = pltpu.get_barrier_semaphore()
 
     def greet(d):
@@ -196,6 +191,14 @@
     def _():
         greet(dest[8])
 
+    loads += fetch(
+        [
+            (pos_any, pos), (spec_any, spec_ref), (edges_any, edges_ref), (count_any, count_ref),
+            (table_any, table_ref), (w1_any, w1_ref), (w2_any, w2_ref), (wout_any, wout_ref),
+        ],
+        lsem,
+        1,
+    )
     for c in loads[1:3]:
         c.wait()
     pack_small(pos, spec_ref, stage, mown)
@@ -220,10 +223,13 @@
             src, dst = src.at[part], dst.at[part]
         return remote(src, dst, fsend, frecv.at[n], to)
 
-    f_g_up = feature(0, feat_ref, 0, dest[0])
-    f_g_dn = feature(1, feat_ref, 1, dest[1])
+    head = pl.ds(0, ROWS - PART)
+    n_parts = len(parts)
+    f_g = [feature(k, feat_ref, k, dest[k], head) for k in range(2)]
+    f_g_last = [feature(6 + n_parts + k, feat_ref, k, dest[k], parts[-1]) for k in range(2)]
+    r_out = [feature(3, fslot.at[k], 6 + k, dest[3], parts[-1]) for k in range(2)]
     f_part = feature(2, feat_ref, 2, dest[2])
-    r_part = [feature(2, fslot.at[0], 4, dest[2]), feature(2, fslot.at[1], 5, dest[2])]
+    r_part = [feature(3, fslot.at[0], 4, dest[2]), feature(3, fslot.at[1], 5, dest[2])]
     r_up = [feature(3, fslot.at[3], 6, dest[0], c) for c in parts]
     r_dn = [feature(3, fslot.at[3], 7, dest[1], c) for c in parts]
     f_p_up = [feature(4, feat_ref, 8, dest[8], pl.ds(ROWS // 2 * k, ROWS // 2)) for k in range(2)]
@@ -236,8 +242,7 @@
 
     meta_sent, feat_sent = of_size(mslot, msend, msend), of_size(fslot, fsend, fsend)
     meta_rest = of_size(mslot.at[pl.ds(3, 7)], msend, mrecv.at[3])
-    near_come = of_size(fslot.at[pl.ds(4, 3)], fsend, frecv.at[2])
-    far_come = of_size(fslot.at[pl.ds(6, 2)], fsend, frecv.at[3])
+    corners = of_size(fslot.at[pl.ds(4, 4)], fsend, frecv.at[3])
     back_all = of_size(pslot, psend, precv)
 
     loads[0].wait()
@@ -260,7 +265,7 @@
         sib_meta.start()
         sib_feat.start()
 
-    direct = ((meta[0], f_g_up), (meta[1], f_g_dn), (meta[2], f_part), (meta[3], *f_out))
+    direct = ((meta[0], f_g_last[0], f_g[0]), (meta[1], f_g_last[1], f_g[1]), (meta[2], f_part), (meta[3], *f_out))
     meta[4].start()
     f_p_up[0].start()
 
@@ -340,22 +345,41 @@
     meta[3].wait_recv()
     m_up.start()
     m_dn.start()
-    for k, c in enumerate(f_out):
+    for k in range(2):
+        meta[k].wait_recv()
+        m_part[k].start()
+    for k, c in enumerate(f_out[:-1]):
         c.wait_recv()
         r_up[k].start()
         r_dn[k].start()
+        if k == 0:
+            for c_last in f_g_last:
+                c_last.wait_recv()
+
+            @pl.when(z != 0)
+            def _():
+                for c_out in r_out:
+                    c_out.start()
+
+    f_out[-1].wait_recv()
+
+    @pl.when(z == 0)
+    def _():
+        r_up[-1].start()
+        r_dn[-1].start()
+
+    def to_partner():
+        for k in range(2):
+            f_g[k].wait_recv()
+            r_part[k].start()
+
     @pl.when(via_lo == 1)
     def _():
         f_p_up[1].start()
 
-    for k, c in enumerate((f_g_up, f_g_dn)):
-        meta[k].wait_recv()
-        m_part[k].start()
-        c.wait_recv()
-        r_part[k].start()
-
     @pl.when(z == 0)
     def _():
+        to_partner()
         sib_meta.wait_recv()
         sib_feat.wait_recv()
         pl.semaphore_wait(ready, 1)
@@ -422,12 +446,14 @@
                     xbuf[start : start + 16, :] = jnp.concatenate(prods[l], 0).astype(BF16)
 
     def last_columns():
-        far_come.wait_recv()
-        gj[...] = gj[...] + dot(jnp.concatenate([fslot[6], fslot[7]], 1), ohc[7 * ATOMS :, :])
-
-    near_come.wait_recv()
-    order = [fslot[0], feat_ref[...], *(fslot[k] for k in range(1, 6))]
-    gj[...] = dot(jnp.concatenate(order, 1), ohc[0 : 7 * ATOMS, :])
+        corners.wait_recv()
+        late_blocks = jnp.concatenate([fslot[k] for k in range(4, 8)], 1)
+        gj[...] = gj[...] + dot(late_blocks, ohc[5 * ATOMS :, :])
+
+    pl.when(z != 0)(to_partner)
+    f_part.wait_recv()
+    order = [fslot[0], feat_ref[...], fslot[1], fslot[2], fslot[3]]
+    gj[...] = dot(jnp.concatenate(order, 1), ohc[0 : 5 * ATOMS, :])
 
     @pl.when(z == 0)
     def _():
@@ -534,13 +560,14 @@
         kernel,
         name="edge_forces",
         out_shape=(pltpu.VMEM((3, 1, ATOMS), F32), pltpu.VMEM((1, EDGES), F32)),
-        in_specs=[*[hbm] * 4, pl.BlockSpec(memory_space=pltpu.SMEM), *[hbm] * 4],
+        in_specs=[hbm] * 9,
         out_specs=(vmem, vmem),
         scratch_shapes=[
             small[0],
             pltpu.VMEM((ROWS, ATOMS), BF16),
             small[1],
             pltpu.VMEM((2, EDGES), jnp.int32),
+            pltpu.SMEM((1, 1), jnp.int32),
             pltpu.VMEM((6, CH), BF16),
             pltpu.VMEM((RB + 5 * CH, LAT), BF16),
             pltpu.VMEM((CH, LAT), BF16),
@@ -569,13 +596,13 @@
             pltpu.VMEM((16, ATOMS), F32),
             pltpu.VMEM((NSLOT, 8, ATOMS), F32),
             pltpu.VMEM((NSLOT, 8, ATOMS), F32),
-            dma((8,)),
+            dma((9,)),
             pltpu.SemaphoreType.REGULAR,
             pltpu.SemaphoreType.REGULAR,
             dma,
             dma((4,)),
             dma,
-            dma((6 + ROWS // PART,)),
+            dma((8 + ROWS // PART,)),
             dma((2,)),
             dma((2,)),
             dma,

time: 39.6 us -> 39.6 us (level)
  no operation moved by 1% of the time
where the time goes in v7:
time: 39.6 us; the launch traced here: 39.4 us
  Pallas kernels  38.1 us (96%)
  between operations  1.29 us (3%)
    pallas_call x1, Pallas kernels, shards(): pl.pallas_call(kernel, name='edge_forces', out_shape=(pltpu.VMEM((3, 1, A...  37.5 us

profile of v7, /device:TPU:1, one launch (start us, length us, event | category | flops | bytes accessed | tf_op | source)
XLA Modules:
  0.0 39.4 jit_solution(16234482167166536160)
XLA Ops:
  1.3 37.5 %edge_forces.1 = (f32[3,1,128]{2,1,0:T(1,128)S(1)}, f32[1,512]{1,0:T(1,128)S(1)}) custom-call(f32[3,1,128]{2,1,0:T(1,128)} %bitcast.15, bf16[576,128]{1,0:T(8,128)(2,1)} %bitcast.12, s32[1,128]{1,0:T(1,128)} %bitcast.16, s32[2,512]{1,0:T(2,128)} %bitcast.14, s32[1,1]{1,0:T(1,128)} %bitcast.11.count_any, bf16[6,64]{1,0:T(8,128)(2,1)} %table_any.1, ...), custom_call_target="tpu_custom_call" | custom-call | tf_op jit(solution)/shard_map/edge_forces/pallas_call | solution.py:559
  38.8 0.6 %finish.1 = (f32[3,1,128]{2,1,0:T(1,128)}, f32[1,512]{1,0:T(1,128)}) custom-call(f32[3,1,128]{2,1,0:T(1,128)S(1)} %get-tuple-element.6.force_ref, f32[1,512]{1,0:T(1,128)S(1)} %get-tuple-element.7.energy_ref), custom_call_target="tpu_custom_call" | custom-call | tf_op jit(solution)/shard_map/finish/pallas_call | solution.py:623

commit v8 on v7

--- a/solution.py
+++ b/solution.py
@@ -13,7 +13,7 @@
 LAT = 128
 RB = 8
 ROWS = 9 * CH
-PART = ROWS // 4
+PART = ROWS // 3
 RADIUS = 3.0
 SOFTEN = 0.04
 F32 = jnp.float32

time: 39.6 us -> 39.6 us (level)
  no operation moved by 1% of the time
where the time goes in v8:
time: 39.6 us; the launch traced here: 39.4 us
  Pallas kernels  38.1 us (96%)
  between operations  1.29 us (3%)
    pallas_call x1, Pallas kernels, shards(): pl.pallas_call(kernel, name='edge_forces', out_shape=(pltpu.VMEM((3, 1, A...  37.5 us

profile of v8, /device:TPU:1, one launch (start us, length us, event | category | flops | bytes accessed | tf_op | source)
XLA Modules:
  0.0 39.4 jit_solution(8785094700493314968)
XLA Ops:
  1.3 37.5 %edge_forces.1 = (f32[3,1,128]{2,1,0:T(1,128)S(1)}, f32[1,512]{1,0:T(1,128)S(1)}) custom-call(f32[3,1,128]{2,1,0:T(1,128)} %bitcast.15, bf16[576,128]{1,0:T(8,128)(2,1)} %bitcast.12, s32[1,128]{1,0:T(1,128)} %bitcast.16, s32[2,512]{1,0:T(2,128)} %bitcast.14, s32[1,1]{1,0:T(1,128)} %bitcast.11.count_any, bf16[6,64]{1,0:T(8,128)(2,1)} %table_any.1, ...), custom_call_target="tpu_custom_call" | custom-call | tf_op jit(solution)/shard_map/edge_forces/pallas_call | solution.py:559
  38.8 0.6 %finish.1 = (f32[3,1,128]{2,1,0:T(1,128)}, f32[1,512]{1,0:T(1,128)}) custom-call(f32[3,1,128]{2,1,0:T(1,128)S(1)} %get-tuple-element.6.force_ref, f32[1,512]{1,0:T(1,128)S(1)} %get-tuple-element.7.energy_ref), custom_call_target="tpu_custom_call" | custom-call | tf_op jit(solution)/shard_map/finish/pallas_call | solution.py:623

commit v9 on v8

--- a/solution.py
+++ b/solution.py
@@ -14,6 +14,7 @@
 RB = 8
 ROWS = 9 * CH
 PART = ROWS // 3
+LOTS = 2
 RADIUS = 3.0
 SOFTEN = 0.04
 F32 = jnp.float32
@@ -422,8 +423,8 @@
     xbuf[5 * CH : 6 * CH - 16, :] = jnp.zeros((CH - 16, EDGES), BF16)
     xbuf[6 * CH - 16 : 6 * CH, :] = jnp.concatenate([jnp.zeros_like(radial), radial], 0).astype(BF16)
 
-    def rows_of(ref, m, k):
-        return ref[m * CH + 8 * k : m * CH + 8 * k + 8, :]
+    def rows_of(ref, m, k, lanes=slice(None)):
+        return ref[m * CH + 8 * k : m * CH + 8 * k + 8, lanes]
 
     def degree_sums(ref, out, other=None):
         for k2 in range(CH // 16):
@@ -474,37 +475,50 @@
         last_columns()
         degree_sums(gj, sj, si)
 
-    z1 = dot(wp[...], xbuf[...])
-    sig1 = 1.0 / (1.0 + jnp.exp(-z1))
-    z2 = dot(w2_ref[...], (z1 * sig1).astype(BF16))
-    sig2 = 1.0 / (1.0 + jnp.exp(-z2))
-    u = jnp.sum(wout * (z2 * sig2), 0, keepdims=True)
-    energy_ref[...] = env * u
-
-    dz2 = (wout * env) * (sig2 * (1.0 + z2 * (1.0 - sig2)))
-    dh = dot(w2t[...], dz2.astype(BF16)).astype(BF16).astype(F32)
-    dz1 = dh * (sig1 * (1.0 + z1 * (1.0 - sig1)))
-    dxv = dot(wpt[...], dz1.astype(BF16)).astype(BF16).astype(F32)
-    acc = [jnp.zeros((8, EDGES), F32) for _ in range(8)]
-    for k in range(CH // 8):
-        for l, ms in ((1, (1, 2, 3)), (2, (4, 5, 6, 7, 8))):
-            at = slice(l * CH + 8 * k, l * CH + 8 * k + 8)
-            dq = dxv[2 * CH + at.start : 2 * CH + at.stop, :]
-            di, dj = dq * sj[at, :], dq * si[at, :]
-            for m in ms:
-                acc[m - 1] = acc[m - 1] + di * rows_of(gi, m, k) + dj * rows_of(gj, m, k)
-    h1, h2, h3, h4, h5, h6, h7, h8 = (jnp.sum(a, 0, keepdims=True) for a in acc)
-    ax = root3 * h1 + root15 * (ny * h4 + nz * h7 + nx * h8)
-    ay = root3 * h2 + root15 * (nx * h4 + nz * h5 - ny * h8)
-    az = root3 * h3 + root15 * (ny * h5 + nx * h7) + (3.0 * root5) * nz * h6
-    dr = jnp.sum(dxv[6 * CH - RB : 6 * CH, :] * slope, 0, keepdims=True)
-    dr = dr - (ax * nx + ay * ny + az * nz) * inv
-    denv = live * u * (2.0 * gap) * (-1.0 / (RADIUS * RADIUS))
-    scale = dr * inv + 2.0 * denv
+    lots = [slice(EDGES // LOTS * h, EDGES // LOTS * (h + 1)) for h in range(LOTS)]
+
+    def cut(a):
+        return [a[:, e] for e in lots]
+
+    def each(fn, *lists):
+        return [fn(*args) for args in zip(*lists)]
+
+    env_, live_, gap_, inv_ = cut(env), cut(live), cut(gap), cut(inv)
+    nx_, ny_, nz_, slope_ = cut(nx), cut(ny), cut(nz), cut(slope)
+    d_ = [cut(dx), cut(dy), cut(dz)]
+    z1 = [dot(wp[...], xbuf[:, e]) for e in lots]
+    sig1 = each(lambda v: 1.0 / (1.0 + jnp.exp(-v)), z1)
+    z2 = each(lambda v, s: dot(w2_ref[...], (v * s).astype(BF16)), z1, sig1)
+    sig2 = each(lambda v: 1.0 / (1.0 + jnp.exp(-v)), z2)
+
+    dz2 = each(lambda v, s, w: (wout * w) * (s * (1.0 + v * (1.0 - s))), z2, sig2, env_)
+    dh = each(lambda v: dot(w2t[...], v.astype(BF16)).astype(BF16).astype(F32), dz2)
+    dz1 = each(lambda d, v, s: d * (s * (1.0 + v * (1.0 - s))), dh, z1, sig1)
+    dxv = each(lambda v: dot(wpt[...], v.astype(BF16)).astype(BF16).astype(F32), dz1)
+    u = each(lambda v, s: jnp.sum(wout * (v * s), 0, keepdims=True), z2, sig2)
+    for h, e in enumerate(lots):
+        energy_ref[:, e] = env_[h] * u[h]
     gbuf[...] = jnp.zeros_like(gbuf)
-    gbuf[0:1, :] = ax * inv + dx * scale
-    gbuf[1:2, :] = ay * inv + dy * scale
-    gbuf[2:3, :] = az * inv + dz * scale
+    for h, e in enumerate(lots):
+        nx, ny, nz, inv = nx_[h], ny_[h], nz_[h], inv_[h]
+        acc = [jnp.zeros((8, EDGES // LOTS), F32) for _ in range(8)]
+        for k in range(CH // 8):
+            for l, ms in ((1, (1, 2, 3)), (2, (4, 5, 6, 7, 8))):
+                at = slice(l * CH + 8 * k, l * CH + 8 * k + 8)
+                dq = dxv[h][2 * CH + at.start : 2 * CH + at.stop, :]
+                di, dj = dq * sj[at, e], dq * si[at, e]
+                for m in ms:
+                    acc[m - 1] = acc[m - 1] + di * rows_of(gi, m, k, e) + dj * rows_of(gj, m, k, e)
+        h1, h2, h3, h4, h5, h6, h7, h8 = (jnp.sum(a, 0, keepdims=True) for a in acc)
+        ax = root3 * h1 + root15 * (ny * h4 + nz * h7 + nx * h8)
+        ay = root3 * h2 + root15 * (nx * h4 + nz * h5 - ny * h8)
+        az = root3 * h3 + root15 * (ny * h5 + nx * h7) + (3.0 * root5) * nz * h6
+        dr = jnp.sum(dxv[h][6 * CH - RB : 6 * CH, :] * slope_[h], 0, keepdims=True)
+        dr = dr - (ax * nx + ay * ny + az * nz) * inv
+        denv = live_[h] * u[h] * (2.0 * gap_[h]) * (-1.0 / (RADIUS * RADIUS))
+        scale = dr * inv + 2.0 * denv
+        for k, a in enumerate((ax, ay, az)):
+            gbuf[k : k + 1, e] = a * inv + d_[k][h] * scale
 
     grad = gbuf[...]
     g_hi = grad.astype(BF16).astype(F32)

time: 39.6 us -> 39.5 us (level)
  no operation moved by 1% of the time
where the time goes in v9:
time: 39.5 us; the launch traced here: 39.4 us
  Pallas kernels  38.1 us (96%)
  between operations  1.29 us (3%)
    pallas_call x1, Pallas kernels, shards(): pl.pallas_call(kernel, name='edge_forces', out_shape=(pltpu.VMEM((3, 1, A...  37.5 us

profile of v9, /device:TPU:1, one launch (start us, length us, event | category | flops | bytes accessed | tf_op | source)
XLA Modules:
  0.0 39.4 jit_solution(1893715658687453276)
XLA Ops:
  1.3 37.5 %edge_forces.1 = (f32[3,1,128]{2,1,0:T(1,128)S(1)}, f32[1,512]{1,0:T(1,128)S(1)}) custom-call(f32[3,1,128]{2,1,0:T(1,128)} %bitcast.15, bf16[576,128]{1,0:T(8,128)(2,1)} %bitcast.12, s32[1,128]{1,0:T(1,128)} %bitcast.16, s32[2,512]{1,0:T(2,128)} %bitcast.14, s32[1,1]{1,0:T(1,128)} %bitcast.11.count_any, bf16[6,64]{1,0:T(8,128)(2,1)} %table_any.1, ...), custom_call_target="tpu_custom_call" | custom-call | tf_op jit(solution)/shard_map/edge_forces/pallas_call | solution.py:573
  38.8 0.6 %finish.1 = (f32[3,1,128]{2,1,0:T(1,128)}, f32[1,512]{1,0:T(1,128)}) custom-call(f32[3,1,128]{2,1,0:T(1,128)S(1)} %get-tuple-element.6.force_ref, f32[1,512]{1,0:T(1,128)S(1)} %get-tuple-element.7.energy_ref), custom_call_target="tpu_custom_call" | custom-call | tf_op jit(solution)/shard_map/finish/pallas_call | solution.py:637
